TPU v7x, 32 devices: a whole 2x2x4 slice. The times are simulated.
32 devices in a mesh: row: 8 (over z, core), loop: 4 (over y, x).
Axes of the slice: x: 2, y: 2, z: 4, core: 2. Of those that a mesh axis runs over, the one named last changes fastest.
Arguments:
- student_image: bfloat16 [5120, 1024], P(('row', 'loop')), may hold values from -12 to 12
- student_text: bfloat16 [5120, 1024], P(('row', 'loop')), may hold values from -12 to 12
- teacher_image: bfloat16 [5120, 1024], P('row', 'loop'), may hold values from -12 to 12
- teacher_text: bfloat16 [5120, 1024], P('row', 'loop'), may hold values from -12 to 12
- student_scale: float32 [1], replicated, may hold values from 30 to 100
- teacher_scale: float32 [1], replicated, may hold values from 30 to 100
Outputs:
- loss: float32 [1], replicated
- grad_image: bfloat16 [5120, 1024], P(('row', 'loop'))
- grad_text: bfloat16 [5120, 1024], P(('row', 'loop'))
All inputs are finite; a program needn't handle non-finite values.
Results may differ from a plain program's by a relative error of at most 0.014.
The roundings to bfloat16 on the way count: a program that leaves them out, or rounds other values in their place, can miss the bound.
Values may be sent and summed in bfloat16 or wider, within the bound.
A program may use at most 128 MiB of HBM per device.

v0:
```python
import functools
import jax
import jax.numpy as jnp
from jax import lax
from jax.experimental import pallas as pl
from jax.experimental.pallas import tpu as pltpu
from jax.sharding import PartitionSpec as P

EPS = 1e-06
F32 = jnp.float32
BF16 = jnp.bfloat16
MESH = pl.DeviceIdType.MESH
STEP = 32
CHUNKS = 2


class Ids:
    def __init__(self):
        self.table = {}
        self.count = 0

    def take(self, name, size=1):
        self.table[name] = self.count
        self.count += size

    def __getitem__(self, name):
        return self.table[name]


def make_ids(n_loop, n_kh, n_kl, n_lx, n_ly):
    ids = Ids()
    ids.take("t_img", n_loop)
    ids.take("t_txt", n_loop)
    for a in range(2):
        ids.take(("iz", a), n_kl * CHUNKS)
        ids.take(("iy", a), n_ly * n_kl * CHUNKS)
        ids.take(("tz", a), n_kh * CHUNKS)
        ids.take(("tx", a), n_lx * n_kh * CHUNKS)
        ids.take(("tc", a), n_lx * n_kh * CHUNKS)
    ids.take("stat", n_kl * n_ly)
    ids.take("dc", n_lx * n_kh * CHUNKS)
    ids.take("dx", n_lx * n_kh * CHUNKS)
    ids.take("dz", n_kh * CHUNKS)
    ids.take("gy", n_ly * n_kl * CHUNKS)
    ids.take("gz", n_kl * CHUNKS)
    ids.take("lk", n_kh)
    ids.take("lx", n_lx)
    ids.take("lc", 1)
    return ids


def kernel(
    dims, ids,
    si, st, ti, tt, ssc, tsc,
    loss_out, gi_out, gt_out,
    img_s, img_t, own_s, own_t, txt_s, txt_t, raw_i, raw_t,
    slog, tlog, grad, stat, dimg_acc, r1, r2, r3, ry, rz, part,
    ss, rs,
):
    n_row, n_loop, n_kh, n_kl, n_lx, n_ly, D, code = dims
    n_img = n_kl * n_ly
    n_txt = n_kh * n_lx * 2
    rows = n_img * D
    Dc = D // CHUNKS
    cols = n_txt * D
    feat = code // n_loop
    r = lax.axis_index("row")
    l = lax.axis_index("loop")
    k, c = r // 2, r % 2
    kh, kl = k // n_kl, k % n_kl
    src_kl, src_j = k // n_kh, k % n_kh
    ly, lx = l // n_lx, l % n_lx
    sscale = ssc[0]
    tscale = tsc[0]

    def dev(k_=None, c_=None, ly_=None, lx_=None):
        kk = k if k_ is None else k_
        cc = c if c_ is None else c_
        yy = ly if ly_ is None else ly_
        xx = lx if lx_ is None else lx_
        return (kk * 2 + cc, yy * n_lx + xx)

    def piece(ref, slot):
        return ref.at[pl.ds(pl.multiple_of(slot * D, D), D), :]

    def chunk(ref, slot, h):
        return ref.at[pl.ds(pl.multiple_of(slot * D + h * Dc, Dc), Dc), :]

    def chunk_of(ref, i, h):
        return ref.at[i, pl.ds(h * Dc, Dc), :]

    def at(slot):
        return pl.ds(pl.multiple_of(slot * D, D), D)

    def copy(src, dst, q_send, q_recv, device):
        return pltpu.make_async_remote_copy(
            src_ref=src, dst_ref=dst, send_sem=ss.at[q_send], recv_sem=rs.at[q_recv],
            device_id=device, device_id_type=MESH,
        )

    sent = []

    def send(src, dst, q_send, q_recv, device):
        op = copy(src, dst, q_send, q_recv, device)
        op.start()
        sent.append(op)

    def got(dst, q):
        copy(dst, dst, q, q, dev(c_=1 - c)).wait_recv()

    def drain():
        for op in sent:
            op.wait_send()
        sent.clear()

    barrier = pltpu.get_barrier_semaphore()
    n_peer = 0
    for d in range(1, n_loop):
        pl.semaphore_signal(barrier, inc=1, device_id=(r, (l + d) % n_loop), device_id_type=MESH)
        n_peer += 1
    for d in range(1, n_kh * n_kl):
        pl.semaphore_signal(barrier, inc=1, device_id=dev(k_=(k + d) % (n_kh * n_kl)), device_id_type=MESH)
        n_peer += 1
    pl.semaphore_signal(barrier, inc=1, device_id=dev(c_=1 - c), device_id_type=MESH)
    n_peer += 1
    for d in range(1, n_kl):
        for e in range(1, n_ly):
            diagonal = dev(k_=kh * n_kl + (kl + d) % n_kl, ly_=(ly + e) % n_ly)
            pl.semaphore_signal(barrier, inc=1, device_id=diagonal, device_id_type=MESH)
            n_peer += 1
    pl.semaphore_wait(barrier, n_peer)

    slot0 = kl * n_ly + ly

    def islot(kl_, ly_):
        return kl_ * n_ly + ly_

    def tslot(j, lx_, c_):
        return (j * n_lx + lx_) * 2 + c_

    def inv_norm(x):
        n2 = jnp.sum(x * x, axis=1, keepdims=True) + EPS
        n = jnp.sqrt(n2)
        return n, 1.0 / n

    HALF = Dc if Dc <= 80 else 16

    def unit_to(src, dst, base, h):
        def body(i, _):
            o = pl.multiple_of(h * Dc + i * HALF, HALF)
            x = src[pl.ds(o, HALF), :].astype(F32)
            _, inv = inv_norm(x)
            dst[pl.ds(pl.multiple_of(base + o, HALF), HALF), :] = (x * inv).astype(BF16)
            return 0
        lax.fori_loop(0, Dc // HALF, body, 0)

    def a2a(src, raw, base):
        for d in range(1, n_loop):
            peer = (l + d) % n_loop
            send(piece(src, peer), raw.at[l], base + d, base + d, (r, peer))

    def image_first(a, buf, h):
        for d in range(1, n_kl):
            p = (kl + d) % n_kl
            q = ids[("iz", a)] + d * CHUNKS + h
            send(chunk(buf, slot0, h), chunk(buf, slot0, h), q, q, dev(k_=kh * n_kl + p))
        for e in range(1, n_ly):
            q = ids[("iy", a)] + e * n_kl * CHUNKS + h
            send(chunk(buf, slot0, h), chunk(buf, slot0, h), q, q, dev(ly_=(ly + e) % n_ly))

    def image_relay(a, buf, h):
        for d in range(1, n_kl):
            s = islot((kl + n_kl - d) % n_kl, ly)
            got(chunk(buf, s, h), ids[("iz", a)] + d * CHUNKS + h)
            for e in range(1, n_ly):
                q = ids[("iy", a)] + (e * n_kl + d) * CHUNKS + h
                send(chunk(buf, s, h), chunk(buf, s, h), q, q, dev(ly_=(ly + e) % n_ly))

    def image_finish(a, buf):
        for h in range(CHUNKS):
            for e in range(1, n_ly):
                for d in range(n_kl):
                    s = islot((kl + n_kl - d) % n_kl, (ly + n_ly - e) % n_ly)
                    got(chunk(buf, s, h), ids[("iy", a)] + (e * n_kl + d) * CHUNKS + h)

    def text_first_copy(a, own, buf, h, g):
        dest = g * n_kl + src_kl
        q = ids[("tz", a)]
        s = tslot(src_j, lx, c)
        op = copy(chunk(own, 0, h), chunk(buf, s, h), q + g * CHUNKS + h,
                  q + src_j * CHUNKS + h, dev(k_=dest))
        return dest, op

    def text_first(a, own, buf, h):
        for g in range(n_kh):
            dest, op = text_first_copy(a, own, buf, h, g)

            @pl.when(dest != k)
            def _():
                op.start()

            @pl.when(dest == k)
            def _():
                o = pl.multiple_of(tslot(src_j, lx, c) * D + h * Dc, Dc)
                buf[pl.ds(o, Dc), :] = own[pl.ds(h * Dc, Dc), :]

    def text_first_drain(a, own, buf):
        for h in range(CHUNKS):
            for g in range(n_kh):
                dest, op = text_first_copy(a, own, buf, h, g)

                @pl.when(dest != k)
                def _():
                    op.wait_send()

    def text_relay(a, buf, h):
        for j in range(n_kh):
            s = tslot(j, lx, c)

            @pl.when(kl * n_kh + j != k)
            def _():
                got(chunk(buf, s, h), ids[("tz", a)] + j * CHUNKS + h)

            for e in range(1, n_lx):
                q = ids[("tx", a)] + (e * n_kh + j) * CHUNKS + h
                send(chunk(buf, s, h), chunk(buf, s, h), q, q, dev(lx_=(lx + e) % n_lx))
            q = ids[("tc", a)] + j * CHUNKS + h
            send(chunk(buf, s, h), chunk(buf, s, h), q, q, dev(c_=1 - c))

    def text_cross(a, buf, h):
        for e in range(1, n_lx):
            for j in range(n_kh):
                s = tslot(j, (lx + n_lx - e) % n_lx, c)
                got(chunk(buf, s, h), ids[("tx", a)] + (e * n_kh + j) * CHUNKS + h)
                q = ids[("tc", a)] + (e * n_kh + j) * CHUNKS + h
                send(chunk(buf, s, h), chunk(buf, s, h), q, q, dev(c_=1 - c))

    def text_finish(a, buf, e):
        for h in range(CHUNKS):
            for j in range(n_kh):
                s = tslot(j, (lx + n_lx - e) % n_lx, 1 - c)
                got(chunk(buf, s, h), ids[("tc", a)] + (e * n_kh + j) * CHUNKS + h)

    def teacher_wait(src, raw, base_id):
        raw[l] = src[at(l), :]
        for d in range(1, n_loop):
            got(raw.at[(l + n_loop - d) % n_loop], base_id + d)

    def teacher_unit(raw, dst, base, h):
        def body(i, _):
            o = pl.multiple_of(h * Dc + i * HALF, HALF)
            xs = [raw[f, pl.ds(o, HALF), :].astype(F32) for f in range(n_loop)]
            x = jnp.concatenate(xs, axis=1)
            _, inv = inv_norm(x)
            dst[pl.ds(pl.multiple_of(base + o, HALF), HALF), :] = (x * inv).astype(BF16)
            return 0
        lax.fori_loop(0, Dc // HALF, body, 0)

    a2a(tt, raw_t, ids["t_txt"])
    a2a(ti, raw_i, ids["t_img"])
    for h in range(CHUNKS):
        unit_to(st, own_s, 0, h)
        text_first(0, own_s, txt_s, h)
        unit_to(si, img_s, slot0 * D, h)
        image_first(0, img_s, h)
    for h in range(CHUNKS):
        if h == 0:
            text_relay(0, txt_s, h)
            image_relay(0, img_s, h)
            teacher_wait(tt, raw_t, ids["t_txt"])
        teacher_unit(raw_t, own_t, 0, h)
        text_first(1, own_t, txt_t, h)
        if h == 0:
            teacher_wait(ti, raw_i, ids["t_img"])
        teacher_unit(raw_i, img_t, slot0 * D, h)
        image_first(1, img_t, h)
    for h in range(1, CHUNKS):
        text_relay(0, txt_s, h)
        image_relay(0, img_s, h)
    for h in range(CHUNKS):
        text_cross(0, txt_s, h)
        text_relay(1, txt_t, h)
        image_relay(1, img_t, h)
    image_finish(0, img_s)
    for e in range(n_lx):
        text_finish(0, txt_s, e)

    TILE = 2 * D

    def logits(txt, img, scale, out, e, m):
        def body(j, m):
            o = pl.multiple_of((j * n_lx + (lx + n_lx - e) % n_lx) * TILE, TILE)
            v = scale * lax.dot_general(
                txt[pl.ds(o, TILE), :], img[...], (((1,), (1,)), ((), ())),
                preferred_element_type=F32,
            )
            out[pl.ds(o, TILE), :] = v
            return jnp.maximum(m, jnp.max(v.reshape(TILE // 8, 8, rows), axis=0))
        return lax.fori_loop(0, n_kh, body, m)

    low = jnp.full((8, rows), -jnp.inf, F32)
    top = low
    for e in range(n_lx):
        top = logits(txt_s, img_s, sscale, slog, e, top)
    smax = jnp.max(top, axis=0, keepdims=True)
    for h in range(CHUNKS):
        text_cross(1, txt_t, h)
    image_finish(1, img_t)
    top = low
    for e in range(n_lx):
        text_finish(1, txt_t, e)
        top = logits(txt_t, img_t, tscale, tlog, e, top)
    tmax = jnp.max(top, axis=0, keepdims=True)

    def exps(i, carry):
        a, b, x = carry
        o = pl.multiple_of(i * STEP, STEP)
        s = slog[pl.ds(o, STEP), :]
        t = tlog[pl.ds(o, STEP), :]
        es = jnp.exp(s - smax)
        et = jnp.exp(t - tmax)
        slog[pl.ds(o, STEP), :] = es
        tlog[pl.ds(o, STEP), :] = et

        def fold(v):
            return jnp.sum(v.reshape(STEP // 8, 8, rows), axis=0)
        return (a + fold(es), b + fold(et), x + fold(et * (t - s)))

    zero = jnp.zeros((8, rows), F32)
    asum, bsum, xsum = lax.fori_loop(0, cols // STEP, exps, (zero, zero, zero))
    pack = [smax, tmax] + [jnp.sum(v, axis=0, keepdims=True) for v in (asum, bsum, xsum)]
    stat[slot0] = jnp.concatenate(pack + [jnp.zeros((3, rows), F32)], axis=0)
    for d in range(n_kl):
        for e in range(n_ly):
            if d or e:
                q = ids["stat"] + d * n_ly + e
                send(stat.at[slot0], stat.at[slot0], q, q,
                     dev(k_=kh * n_kl + (kl + d) % n_kl, ly_=(ly + e) % n_ly))
    for d in range(n_kl):
        for e in range(n_ly):
            if d or e:
                s = islot((kl + n_kl - d) % n_kl, (ly + n_ly - e) % n_ly)
                got(stat.at[s], ids["stat"] + d * n_ly + e)

    all_stat = [stat[s] for s in range(n_img)]
    gs = functools.reduce(jnp.maximum, [v[0:1] for v in all_stat])
    gt = functools.reduce(jnp.maximum, [v[1:2] for v in all_stat])
    es = [jnp.exp(v[0:1] - gs) for v in all_stat]
    et = [jnp.exp(v[1:2] - gt) for v in all_stat]
    ssum = sum(v[2:3] * e for v, e in zip(all_stat, es))
    tsum = sum(v[3:4] * e for v, e in zip(all_stat, et))
    cross = sum(v[4:5] * e for v, e in zip(all_stat, et))
    diverge = cross / tsum - (gt + jnp.log(tsum)) + (gs + jnp.log(ssum))
    s_mul = sscale * jnp.exp(smax - gs) / ssum
    t_mul = sscale * jnp.exp(tmax - gt) / tsum

    def to_grad(i, _):
        o = pl.multiple_of(i * STEP, STEP)
        v = slog[pl.ds(o, STEP), :] * s_mul - tlog[pl.ds(o, STEP), :] * t_mul
        grad[pl.ds(o, STEP), :] = v.astype(BF16)
        return 0
    lax.fori_loop(0, cols // STEP, to_grad, 0)

    drain()
    for a, own, buf in ((0, own_s, txt_s), (1, own_t, txt_t)):
        text_first_drain(a, own, buf)
    dtxt = txt_t

    def dtxt_pieces(lx_, c_):
        def body(j, _):
            rng = at(tslot(j, lx_, c_))
            dtxt[rng, :] = jnp.dot(grad[rng, :], img_s[...], preferred_element_type=F32).astype(BF16)
            return 0
        lax.fori_loop(0, n_kh, body, 0)

    def to_core(e):
        x_ = (lx + e) % n_lx
        dtxt_pieces(x_, 1 - c)
        for h in range(CHUNKS):
            for j in range(n_kh):
                q = ids["dc"] + (e * n_kh + j) * CHUNKS + h
                send(chunk(dtxt, tslot(j, x_, 1 - c), h), chunk_of(r1, x_ * n_kh + j, h), q, q, dev(c_=1 - c))

    def chunk_rows(slot, h):
        return pl.ds(pl.multiple_of(slot * D + h * Dc, Dc), Dc)

    half = [pl.ds(h * Dc, Dc) for h in range(CHUNKS)]

    for e in range(1, n_lx):
        x_ = (lx + e) % n_lx
        to_core(e)
        dtxt_pieces(x_, c)
        if e == n_lx - 1:
            to_core(0)
        for h in range(CHUNKS):
            for j in range(n_kh):
                i = x_ * n_kh + j
                got(chunk_of(r1, i, h), ids["dc"] + (e * n_kh + j) * CHUNKS + h)
                rng = chunk_rows(tslot(j, x_, c), h)
                dtxt[rng, :] = (dtxt[rng, :].astype(F32) + r1[i, half[h], :].astype(F32)).astype(BF16)
                q = ids["dx"] + (e * n_kh + j) * CHUNKS + h
                send(chunk(dtxt, tslot(j, x_, c), h), chunk_of(r2, (e - 1) * n_kh + j, h), q, q, dev(lx_=x_))

    KT = 256
    dimg_acc[...] = jnp.zeros_like(dimg_acc)

    def dimg_body(i, _):
        o = pl.multiple_of(i * KT, KT)
        dimg_acc[...] += lax.dot_general(
            grad[pl.ds(o, KT), :], txt_s[pl.ds(o, KT), :], (((0,), (0,)), ((), ())),
            preferred_element_type=F32,
        )
        return 0
    lax.fori_loop(0, cols // KT, dimg_body, 0)
    dimg = img_t
    for s in range(n_img):
        dimg[pl.ds(s * D, D), :] = dimg_acc[pl.ds(s * D, D), :].astype(BF16)
    for d in [*range(1, n_kl), 0]:
        for h in range(CHUNKS):
            for e in range(1, n_ly):
                y_ = (ly + e) % n_ly
                q = ids["gy"] + (e * n_kl + d) * CHUNKS + h
                send(chunk(dimg, islot((kl + d) % n_kl, y_), h), chunk_of(ry, (e - 1) * n_kl + d, h), q, q, dev(ly_=y_))


    dtxt_pieces(lx, c)

    def owner_copy(j, h):
        dest = kl * n_kh + j
        op = copy(chunk(dtxt, tslot(j, lx, c), h), chunk_of(r3, kh, h),
                  ids["dz"] + j * CHUNKS + h, ids["dz"] + kh * CHUNKS + h, dev(k_=dest))
        return dest, op

    def text_sum(j, h):
        got(chunk_of(r1, lx * n_kh + j, h), ids["dc"] + j * CHUNKS + h)
        rng = chunk_rows(tslot(j, lx, c), h)
        v = dtxt[rng, :].astype(F32) + r1[lx * n_kh + j, half[h], :].astype(F32)
        for e in range(1, n_lx):
            got(chunk_of(r2, (e - 1) * n_kh + j, h), ids["dx"] + (e * n_kh + j) * CHUNKS + h)
            v = v + r2[(e - 1) * n_kh + j, half[h], :].astype(F32)
        dtxt[rng, :] = v.astype(BF16)
        dest, op = owner_copy(j, h)

        @pl.when(dest != k)
        def _():
            op.start()

        @pl.when(dest == k)
        def _():
            r3[kh, half[h], :] = dtxt[rng, :]

    def got_y(d, h):
        for e in range(1, n_ly):
            got(chunk_of(ry, (e - 1) * n_kl + d, h), ids["gy"] + (e * n_kl + d) * CHUNKS + h)

    def image_sum(d, h):
        got_y(d, h)
        pair_slot = islot((kl + d) % n_kl, ly)
        rng = chunk_rows(pair_slot, h)
        v = dimg[rng, :].astype(F32)
        for e in range(1, n_ly):
            v = v + ry[(e - 1) * n_kl + d, half[h], :].astype(F32)
        dimg[rng, :] = v.astype(BF16)
        q = ids["gz"] + d * CHUNKS + h
        send(chunk(dimg, pair_slot, h), chunk_of(rz, d - 1, h), q, q, dev(k_=kh * n_kl + (kl + d) % n_kl))

    for h in range(CHUNKS):
        for j in range(n_kh):
            text_sum(j, h)
        for d in range(1, n_kl):
            image_sum(d, h)
    for h in range(CHUNKS):
        got_y(0, h)

    total = jnp.broadcast_to(jnp.sum(diverge, axis=1, keepdims=True), (8, 128))
    part[kh] = total
    for d in range(1, n_kh):
        q = ids["lk"] + d
        send(part.at[kh], part.at[kh], q, q, dev(k_=((kh + d) % n_kh) * n_kl + kl))
    for d in range(1, n_kh):
        got(part.at[(kh + n_kh - d) % n_kh], ids["lk"] + d)
    base = n_kh
    total = sum(part[i] for i in range(n_kh))
    part[base + lx] = total
    for d in range(1, n_lx):
        q = ids["lx"] + d
        send(part.at[base + lx], part.at[base + lx], q, q, dev(lx_=(lx + d) % n_lx))
    for d in range(1, n_lx):
        got(part.at[base + (lx + n_lx - d) % n_lx], ids["lx"] + d)
    total = sum(part[base + i] for i in range(n_lx))
    base = n_kh + n_lx
    part[base + c] = total
    send(part.at[base + c], part.at[base + c], ids["lc"], ids["lc"], dev(c_=1 - c))
    got(part.at[base + 1 - c], ids["lc"])
    total = part[base] + part[base + 1]
    loss_out[...] = total / float(D * n_row * n_loop)

    def add_terms(terms, out):
        def body(i, _):
            rng = pl.ds(pl.multiple_of(i * HALF, HALF), HALF)
            out[rng, :] = terms(rng)
            return 0
        lax.fori_loop(0, D // HALF, body, 0)

    for d in range(1, n_kl):
        for h in range(CHUNKS):
            got(chunk_of(rz, d - 1, h), ids["gz"] + d * CHUNKS + h)

    def image_terms(rng):
        o = pl.multiple_of(slot0 * D + rng.start, HALF)
        v = dimg[pl.ds(o, HALF), :].astype(F32)
        for e in range(1, n_ly):
            v = v + ry[(e - 1) * n_kl, rng, :].astype(F32)
        for d in range(1, n_kl):
            v = v + rz[d - 1, rng, :].astype(F32)
        return v
    add_terms(image_terms, gi_out)

    for g in range(n_kh):
        @pl.when(g * n_kl + src_kl != k)
        def _():
            for h in range(CHUNKS):
                got(chunk_of(r3, g, h), ids["dz"] + g * CHUNKS + h)
    add_terms(lambda rng: sum(r3[g, rng, :].astype(F32) for g in range(n_kh)), gt_out)

    drain()
    for j in range(n_kh):
        for h in range(CHUNKS):
            dest, op = owner_copy(j, h)

            @pl.when(dest != k)
            def _():
                op.wait_send()


def back_norms(si, st, total, di, dt, loss_out, gi_out, gt_out):
    loss_out[0] = total[0, 0]
    D = si.shape[0]
    block = 32 if D % 32 == 0 else 16

    def body(i, _):
        rng = pl.ds(pl.multiple_of(i * block, block), block)
        for src, grad_unit, out in ((si, di, gi_out), (st, dt, gt_out)):
            x = src[rng, :].astype(F32)
            g = grad_unit[rng, :]
            inv = 1.0 / jnp.sqrt(jnp.sum(x * x, axis=1, keepdims=True) + EPS)
            along = jnp.sum(g * x, axis=1, keepdims=True) * inv * inv
            out[rng, :] = ((g - x * along) * inv).astype(BF16)
        return 0
    lax.fori_loop(0, D // block, body, 0, unroll=True)


def on_device(n_row, n_loop, si, st, ti, tt, ssc, tsc):
    D, code = si.shape
    n_kl, n_lx = 2, 2
    n_kh, n_ly = n_row // (2 * n_kl), n_loop // n_lx
    n_img, n_txt = n_kl * n_ly, n_kh * n_lx * 2
    rows, cols = n_img * D, n_txt * D
    ids = make_ids(n_loop, n_kh, n_kl, n_lx, n_ly)
    dims = (n_row, n_loop, n_kh, n_kl, n_lx, n_ly, D, code)
    vm = pl.BlockSpec(memory_space=pltpu.VMEM)
    sm = pl.BlockSpec(memory_space=pltpu.SMEM)
    V = pltpu.VMEM
    loss, gi, gt = pl.pallas_call(
        functools.partial(kernel, dims, ids),
        out_shape=(
            jax.ShapeDtypeStruct((8, 128), F32),
            jax.ShapeDtypeStruct((D, code), F32),
            jax.ShapeDtypeStruct((D, code), F32),
        ),
        in_specs=[vm] * 4 + [sm] * 2,
        out_specs=(vm, vm, vm),
        scratch_shapes=[
            V((rows, code), BF16), V((rows, code), BF16),
            V((D, code), BF16), V((D, code), BF16),
            V((cols, code), BF16), V((cols, code), BF16),
            V((n_loop, D, code // n_loop), BF16), V((n_loop, D, code // n_loop), BF16),
            V((cols, rows), F32), V((cols, rows), F32), V((cols, rows), BF16),
            V((n_img, 8, rows), F32),
            V((rows, code), F32),
            V((n_lx * n_kh, D, code), BF16),
            V(((n_lx - 1) * n_kh, D, code), BF16),
            V((n_kh, D, code), BF16),
            V(((n_ly - 1) * n_kl, D, code), BF16),
            V((n_kl - 1, D, code), BF16),
            V((n_kh + n_lx + 2, 8, 128), F32),
            pltpu.SemaphoreType.DMA((ids.count,)),
            pltpu.SemaphoreType.DMA((ids.count,)),
        ],
        compiler_params=pltpu.CompilerParams(
            collective_id=0, has_side_effects=True, vmem_limit_bytes=67043328,
        ),
    )(si, st, ti, tt, ssc, tsc)
    return pl.pallas_call(
        back_norms,
        out_shape=(
            jax.ShapeDtypeStruct((1,), F32),
            jax.ShapeDtypeStruct((D, code), BF16),
            jax.ShapeDtypeStruct((D, code), BF16),
        ),
        in_specs=[vm] * 5,
        out_specs=(sm, vm, vm),
    )(si, st, loss, gi, gt)


def solution(mesh):
    return jax.shard_map(
        functools.partial(on_device, mesh.shape["row"], mesh.shape["loop"]),
        mesh=mesh,
        in_specs=(
            P(("row", "loop"), None),
            P(("row", "loop"), None),
            P("row", "loop"),
            P("row", "loop"),
            P(),
            P(),
        ),
        out_specs=(P(), P(("row", "loop"), None), P(("row", "loop"), None)),
        check_vma=False,
    )
```

profile of v0, /device:TPU:21, one launch (start us, length us, event | category | flops | bytes accessed | tf_op | source)
XLA Modules:
  0.0 90.6 jit_solution(7098716617414851353)
XLA Ops:
  1.9 85.9 %shard_map.85 = (f32[8,128]{1,0:T(8,128)}, f32[160,1024]{1,0:T(8,128)}, f32[160,1024]{1,0:T(8,128)}) custom-call(bf16[160,1024]{1,0:T(8,128)(2,1)} %si.3, bf16[160,1024]{1,0:T(8,128)(2,1)} %st.3, bf16[640,256]{1,0:T(8,128)(2,1)} %ti.1, bf16[640,256]{1,0:T(8,128)(2,1)} %tt.1, f32[1]{0:T(128)S(6)} %copy.9.ssc, f32[1]{0:T(128)S(6)} %copy.10.tsc), custom_call_target="tpu_custom_call" | custom-call | tf_op jit(solution)/shard_map/pallas_call | solution.py:564
  87.9 2.8 %shard_map.86 = (f32[1]{0:T(128)}, bf16[160,1024]{1,0:T(8,128)(2,1)}, bf16[160,1024]{1,0:T(8,128)(2,1)}) custom-call(bf16[160,1024]{1,0:T(8,128)(2,1)} %si.3, bf16[160,1024]{1,0:T(8,128)(2,1)} %st.3, f32[8,128]{1,0:T(8,128)} %get-tuple-element.6.total, f32[160,1024]{1,0:T(8,128)} %get-tuple-element.7.di, f32[160,1024]{1,0:T(8,128)} %get-tuple-element.8.dt), custom_call_target="tpu_custom_call" | custom-call | tf_op jit(solution)/shard_map/pallas_call | solution.py:594
where the time goes:
time: 90.8 us; the launch traced here: 90.6 us
  Pallas kernels  88.7 us (98%)
  between operations  1.93 us (2%)
    pallas_call x1, Pallas kernels, on_device(): pl.pallas_call(functools.partial(kernel, dims, ids), out_shape=(jax.Shape...  85.9 us
    pallas_call x1, Pallas kernels, on_device(): pl.pallas_call(back_norms, out_shape=(jax.ShapeDtypeStruct((1,), F32), ja...  2.77 us

commit v1 on v0

v1 whole, which is shorter than its diff:
```python
import functools
import jax
import jax.numpy as jnp
from jax import lax
from jax.experimental import pallas as pl
from jax.experimental.pallas import tpu as pltpu
from jax.sharding import PartitionSpec as P

EPS = 1e-06
F32 = jnp.float32
BF16 = jnp.bfloat16
MESH = pl.DeviceIdType.MESH
PART = 64
UNIT = 32
STEP = 32


class Ids:
    def __init__(self):
        self.table = {}
        self.count = 0

    def take(self, name, size=1):
        self.table[name] = self.count
        self.count += size

    def __getitem__(self, name):
        return self.table[name]


def chunk_sizes(D):
    sizes = [PART] * (D // PART)
    if D % PART:
        sizes.append(D % PART)
    return sizes


def make_ids(H, n_kh, n_kl, n_lx, n_ly):
    recv, sent = Ids(), Ids()
    recv.take("t_img")
    recv.take("t_txt")
    for a in range(2):
        recv.take(("iz", a), n_kl * H)
        recv.take(("iy", a), H)
        recv.take(("tz", a), n_kh * H)
        recv.take(("tx", a), n_lx * H)
        recv.take(("tc", a), H)
    recv.take("stat")
    recv.take("dc", n_lx * n_kh)
    recv.take("dx", n_lx * n_kh * H)
    recv.take("dz")
    recv.take("gy", n_kl * H)
    recv.take("gz")
    for name in ("lk", "lx", "lc"):
        recv.take(name)
    for name in ("t_img", "t_txt", "stat", "dc", "dx", "dz", "gy", "gz", "loss"):
        sent.take(name)
    for a in range(2):
        for kind in ("img", "first", "txt"):
            sent.take((kind, a))
    return recv, sent


def kernel(
    dims, rid, sid,
    si, st, ti, tt, ssc, tsc,
    loss_out, gi_out, gt_out,
    img_s, img_t, own_s, own_t, txt_s, txt_t, raw_i, raw_t,
    slog, tlog, grad, stat, acc, r1, r2, r3, ry, rz, part, inv_i, inv_t,
    ss, rs,
):
    n_row, n_loop, n_kh, n_kl, n_lx, n_ly, D, code = dims
    sizes = chunk_sizes(D)
    H = len(sizes)
    off = [sum(sizes[:h]) for h in range(H)]
    n_img = n_kl * n_ly
    n_txt = n_kh * n_lx * 2
    rows = n_img * D
    cols = n_txt * D
    r = lax.axis_index("row")
    l = lax.axis_index("loop")
    k, c = r // 2, r % 2
    kh, kl = k // n_kl, k % n_kl
    src_kl, src_j = k // n_kh, k % n_kh
    ly, lx = l // n_lx, l % n_lx
    sscale = ssc[0]
    tscale = tsc[0]

    def dev(k_=None, c_=None, ly_=None, lx_=None):
        kk = k if k_ is None else k_
        cc = c if c_ is None else c_
        yy = ly if ly_ is None else ly_
        xx = lx if lx_ is None else lx_
        return (kk * 2 + cc, yy * n_lx + xx)

    def islot(kl_, ly_):
        return ly_ * n_kl + kl_

    def tslot(j, lx_, c_):
        return (j * n_lx + lx_) * 2 + c_

    def span(start, size, step):
        return pl.ds(pl.multiple_of(start, step), size)

    def irng(h, slot):
        return span(n_img * off[h] + slot * sizes[h], sizes[h], UNIT)

    def trng(h, slot):
        return span(n_txt * off[h] + slot * sizes[h], sizes[h], UNIT)

    def srng(slot, h):
        return span(slot * D + off[h], sizes[h], UNIT)

    def at(slot):
        return span(slot * D, D, UNIT)

    half = [pl.ds(off[h], sizes[h]) for h in range(H)]

    def copy(src, dst, q_send, q_recv, device):
        return pltpu.make_async_remote_copy(
            src_ref=src, dst_ref=dst, send_sem=ss.at[q_send], recv_sem=rs.at[q_recv],
            device_id=device, device_id_type=MESH,
        )

    sent_rows = {}

    def send(src, dst, name, q, device, n=0):
        copy(src, dst, sid[name], q, device).start()
        sent_rows[name] = sent_rows.get(name, 0) + n

    def got(dst, q):
        copy(dst, dst, 0, q, dev(c_=1 - c)).wait_recv()

    def got_rows(n, q):
        got(txt_s.at[pl.ds(0, n), :], q)

    def left(ref, q):
        copy(ref, ref, q, 0, dev(c_=1 - c)).wait_send()

    def left_rows(*names):
        for name in names:
            left(txt_s.at[pl.ds(0, sent_rows.pop(name)), :], sid[name])

    barrier = pltpu.get_barrier_semaphore()
    n_peer = 0
    for d in range(1, n_loop):
        pl.semaphore_signal(barrier, inc=1, device_id=(r, (l + d) % n_loop), device_id_type=MESH)
        n_peer += 1
    for d in range(1, n_kh * n_kl):
        pl.semaphore_signal(barrier, inc=1, device_id=dev(k_=(k + d) % (n_kh * n_kl)), device_id_type=MESH)
        n_peer += 1
    pl.semaphore_signal(barrier, inc=1, device_id=dev(c_=1 - c), device_id_type=MESH)
    n_peer += 1
    for d in range(1, n_kl):
        for e in range(1, n_ly):
            diagonal = dev(k_=kh * n_kl + (kl + d) % n_kl, ly_=(ly + e) % n_ly)
            pl.semaphore_signal(barrier, inc=1, device_id=diagonal, device_id_type=MESH)
            n_peer += 1

    slot0 = islot(kl, ly)

    def unit(load, dst, first, n, keep=None):
        for o in range(0, n, UNIT):
            x = load(o)
            n2 = jnp.sum(x * x, axis=1, keepdims=True) + EPS
            inv = 1.0 / jnp.sqrt(n2)
            if keep is not None:
                keep(o, inv)
            dst[span(first + o, UNIT, UNIT), :] = (x * inv).astype(BF16)

    def student_unit(src, dst, first, h, inv_ref):
        def load(o):
            return src[pl.ds(off[h] + o, UNIT), :].astype(F32)

        def keep(o, inv):
            inv_ref[pl.ds(off[h] + o, UNIT), :] = jnp.broadcast_to(inv, (UNIT, 128))
        unit(load, dst, first, sizes[h], keep)

    def own_text(h):
        student_unit(st, own_s, off[h], h, inv_t)

    def own_image(h):
        student_unit(si, img_s, n_img * off[h] + slot0 * sizes[h], h, inv_i)

    own_text(0)
    own_image(0)
    pl.semaphore_wait(barrier, n_peer)

    def a2a(src, raw, name):
        for d in range(1, n_loop):
            peer = (l + d) % n_loop
            send(src.at[at(peer), :], raw.at[l], name, rid[name], (r, peer))

    def image_first(a, buf, h):
        rng = irng(h, slot0)
        for d in range(1, n_kl):
            q = rid[("iz", a)] + d * H + h
            send(buf.at[rng, :], buf.at[rng, :], ("img", a), q, dev(k_=kh * n_kl + (kl + d) % n_kl), sizes[h])
        for e in range(1, n_ly):
            send(buf.at[rng, :], buf.at[rng, :], ("img", a), rid[("iy", a)] + h, dev(ly_=(ly + e) % n_ly), sizes[h])

    def image_relay(a, buf, h):
        for d in range(1, n_kl):
            rng = irng(h, islot((kl + n_kl - d) % n_kl, ly))
            got(buf.at[rng, :], rid[("iz", a)] + d * H + h)
            for e in range(1, n_ly):
                send(buf.at[rng, :], buf.at[rng, :], ("img", a), rid[("iy", a)] + h, dev(ly_=(ly + e) % n_ly), sizes[h])

    def image_finish(a, h):
        got_rows((n_ly - 1) * n_kl * sizes[h], rid[("iy", a)] + h)

    def text_first(a, own, buf, h):
        rng = trng(h, tslot(src_j, lx, c))
        for g in range(n_kh):
            dest = g * n_kl + src_kl
            op = copy(own.at[half[h], :], buf.at[rng, :], sid[("first", a)],
                      rid[("tz", a)] + src_j * H + h, dev(k_=dest))

            @pl.when(dest != k)
            def _():
                op.start()

            @pl.when(dest == k)
            def _():
                buf[rng, :] = own[half[h], :]

    def first_left(a):
        @pl.when(src_kl == kl)
        def _():
            left(txt_s.at[pl.ds(0, (n_kh - 1) * D), :], sid[("first", a)])

        @pl.when(src_kl != kl)
        def _():
            left(txt_s.at[pl.ds(0, n_kh * D), :], sid[("first", a)])

    def text_relay(a, buf, h):
        for j in range(n_kh):
            rng = trng(h, tslot(j, lx, c))

            @pl.when(kl * n_kh + j != k)
            def _():
                got(buf.at[rng, :], rid[("tz", a)] + j * H + h)

            for e in range(1, n_lx):
                send(buf.at[rng, :], buf.at[rng, :], ("txt", a), rid[("tx", a)] + e * H + h,
                     dev(lx_=(lx + e) % n_lx), sizes[h])
            send(buf.at[rng, :], buf.at[rng, :], ("txt", a), rid[("tc", a)] + h, dev(c_=1 - c), sizes[h])

    def text_cross(a, buf, h):
        for e in range(1, n_lx):
            got_rows(n_kh * sizes[h], rid[("tx", a)] + e * H + h)
            for j in range(n_kh):
                rng = trng(h, tslot(j, (lx + n_lx - e) % n_lx, c))
                send(buf.at[rng, :], buf.at[rng, :], ("txt", a), rid[("tc", a)] + h, dev(c_=1 - c), sizes[h])

    def text_finish(a, h):
        got_rows(n_lx * n_kh * sizes[h], rid[("tc", a)] + h)

    def teacher_wait(src, raw, name):
        raw[l] = src[at(l), :]
        got(raw.at[pl.ds(0, n_loop - 1)], rid[name])

    def teacher_unit(raw, dst, first, h):
        def load(o):
            xs = [raw[f, pl.ds(off[h] + o, UNIT), :].astype(F32) for f in range(n_loop)]
            return jnp.concatenate(xs, axis=1)
        unit(load, dst, first, sizes[h])

    a2a(tt, raw_t, "t_txt")
    a2a(ti, raw_i, "t_img")
    for h in range(H):
        if h:
            own_text(h)
        text_first(0, own_s, txt_s, h)
        if h:
            own_image(h)
        image_first(0, img_s, h)
    text_relay(0, txt_s, 0)
    image_relay(0, img_s, 0)
    teacher_wait(tt, raw_t, "t_txt")
    for h in range(H):
        teacher_unit(raw_t, own_t, off[h], h)
        text_first(1, own_t, txt_t, h)
        if h == 0:
            teacher_wait(ti, raw_i, "t_img")
        teacher_unit(raw_i, img_t, n_img * off[h] + slot0 * sizes[h], h)
        image_first(1, img_t, h)
    for h in range(1, H):
        text_relay(0, txt_s, h)
        image_relay(0, img_s, h)
    for h in range(H):
        text_cross(0, txt_s, h)
        if h == 0:
            text_relay(1, txt_t, 0)
            image_relay(1, img_t, 0)
    for h in range(H):
        image_finish(0, h)
        text_finish(0, h)

    TILE = 256

    def logits(txt, img, scale, out, row0, n, lane0, width):
        lanes = pl.ds(lane0, width)

        def body(i, m):
            o = pl.multiple_of(row0 + i * TILE, TILE)
            v = scale * lax.dot_general(
                txt[pl.ds(o, TILE), :], img[lanes, :], (((1,), (1,)), ((), ())),
                preferred_element_type=F32,
            )
            out[pl.ds(o, TILE), lanes] = v
            return jnp.maximum(m, jnp.max(v.reshape(TILE // 8, 8, width), axis=0))
        m = lax.fori_loop(0, n // TILE, body, jnp.full((8, width), -jnp.inf, F32))
        return jnp.max(m, axis=0, keepdims=True)

    smax = logits(txt_s, img_s, sscale, slog, 0, cols, 0, rows)

    def exps(row0, n, lane0, width, tmax):
        lanes = pl.ds(lane0, width)
        top_s = smax[:, lane0:lane0 + width]

        def fold(v):
            return jnp.sum(v.reshape(STEP // 8, 8, width), axis=0)

        def body(i, carry):
            a, b, x = carry
            o = pl.multiple_of(row0 + i * STEP, STEP)
            s = slog[pl.ds(o, STEP), lanes]
            t = tlog[pl.ds(o, STEP), lanes]
            es = jnp.exp(s - top_s)
            et = jnp.exp(t - tmax)
            slog[pl.ds(o, STEP), lanes] = es
            tlog[pl.ds(o, STEP), lanes] = et
            return (a + fold(es), b + fold(et), x + fold(et * (t - s)))
        zero = jnp.zeros((8, width), F32)
        sums = lax.fori_loop(0, n // STEP, body, (zero, zero, zero), unroll=2)
        return [jnp.sum(v, axis=0, keepdims=True) for v in sums]

    lane0 = [n_img * o for o in off]
    width = [n_img * s for s in sizes]
    row0 = [n_txt * o for o in off]
    height = [n_txt * s for s in sizes]
    tops = {}
    sums = {}

    def group(h, hi):
        first = 0 if h == hi else row0[h]
        n = row0[h] + height[h] - first
        m = logits(txt_t, img_t, tscale, tlog, first, n, lane0[hi], width[hi])
        tops[h, hi] = m
        sums[h, hi] = exps(first, n, lane0[hi], width[hi], m)

    def arrive(h):
        text_cross(1, txt_t, h)
        image_finish(1, h)
        text_finish(1, h)
        for hi in range(h):
            group(h, hi)
        group(h, h)

    for h in range(1, H):
        text_relay(1, txt_t, h)
        image_relay(1, img_t, h)
        if h < H - 1:
            arrive(h - 1)
    for h in range(max(H - 2, 0), H):
        arrive(h)

    best = [functools.reduce(jnp.maximum, [tops[h, hi] for h in range(hi, H)]) for hi in range(H)]

    def wide(parts):
        return jnp.concatenate(parts, axis=1)

    def total(i, hi):
        return sum(sums[h, hi][i] * jnp.exp(tops[h, hi] - best[hi]) for h in range(hi, H))
    asum = wide([sum(sums[h, hi][0] for h in range(hi, H)) for hi in range(H)])
    tmax = wide(best)
    bsum = wide([total(1, hi) for hi in range(H)])
    xsum = wide([total(2, hi) for hi in range(H)])
    pack = [smax, tmax, asum, bsum, xsum]
    stat[slot0] = jnp.concatenate(pack + [jnp.zeros((3, rows), F32)], axis=0)
    for d in range(n_kl):
        for e in range(n_ly):
            if d or e:
                send(stat.at[slot0], stat.at[slot0], "stat", rid["stat"],
                     dev(k_=kh * n_kl + (kl + d) % n_kl, ly_=(ly + e) % n_ly))
    for a in range(2):
        first_left(a)
        left_rows(("img", a), ("txt", a))
    got(stat.at[pl.ds(0, n_img - 1)], rid["stat"])

    all_stat = [stat[s] for s in range(n_img)]
    gs = functools.reduce(jnp.maximum, [v[0:1] for v in all_stat])
    gt = functools.reduce(jnp.maximum, [v[1:2] for v in all_stat])
    es = [jnp.exp(v[0:1] - gs) for v in all_stat]
    et = [jnp.exp(v[1:2] - gt) for v in all_stat]
    ssum = sum(v[2:3] * e for v, e in zip(all_stat, es))
    tsum = sum(v[3:4] * e for v, e in zip(all_stat, et))
    s_mul = sscale * jnp.exp(smax - gs) / ssum
    t_scale = sscale / tsum

    def t_factor(h):
        m = wide([tops[max(h, hi), hi] for hi in range(H)])
        return t_scale * jnp.exp(m - gt)
    t_mul = [t_factor(h) for h in range(H)]

    dtxt = txt_t

    def grad_of(rng, h):
        v = (slog[rng, :] * s_mul - tlog[rng, :] * t_mul[h]).astype(BF16)
        grad[rng, :] = v
        return v

    def text_piece(j, lx_, c_, fresh=False):
        slot = tslot(j, lx_, c_)
        if fresh:
            g = [grad_of(trng(h, slot), h) for h in range(H)]
        else:
            g = [grad[trng(h, slot), :] for h in range(H)]
        v = jnp.dot(jnp.concatenate(g, axis=0), img_s[...], preferred_element_type=F32)
        dtxt[at(slot), :] = v.astype(BF16)

    def to_core(j, x_, q):
        send(dtxt.at[at(tslot(j, x_, 1 - c)), :], r1.at[x_ * n_kh + j], "dc", q, dev(c_=1 - c), D)

    order = [(n_kh - 1 - kh + i) % n_kh for i in range(n_kh)]

    def to_x(e, i):
        x_ = (lx + e) % n_lx
        j = order[i]
        s = x_ * n_kh + j
        got(r1.at[s], rid["dc"] + e * n_kh + i)
        for h in range(H):
            rng = srng(tslot(j, x_, c), h)
            dtxt[rng, :] = (dtxt[rng, :].astype(F32) + r1[s, half[h], :].astype(F32)).astype(BF16)
            q = rid["dx"] + (e * n_kh + i) * H + h
            send(dtxt.at[rng, :], r2.at[(e - 1) * n_kh + j, half[h], :], "dx", q, dev(lx_=x_), sizes[h])

    dimg = img_t
    full = [h for h in range(H) if (n_kl * sizes[h]) % 128 == 0]
    rest = [h for h in range(H) if h not in full]
    KT = 256

    def image_piece(y_, with_rest):
        windows = [pl.ds(pl.multiple_of(lane0[h] + y_ * n_kl * sizes[h], 128), n_kl * sizes[h]) for h in full]
        lens = [n_kl * sizes[h] for h in full]
        if with_rest:
            windows += [pl.ds(lane0[h], width[h]) for h in rest]
            lens += [width[h] for h in rest]
        M = sum(lens)

        def body(i, _):
            o = pl.multiple_of(i * KT, KT)
            g = jnp.concatenate([grad[pl.ds(o, KT), w] for w in windows], axis=1)
            v = lax.dot_general(g, txt_s[pl.ds(o, KT), :], (((0,), (0,)), ((), ())), preferred_element_type=F32)

            @pl.when(i == 0)
            def _():
                acc[pl.ds(0, M), :] = v

            @pl.when(i != 0)
            def _():
                acc[pl.ds(0, M), :] += v
            return 0
        lax.fori_loop(0, cols // KT, body, 0)
        o = 0
        for h in full:
            for p in range(n_kl):
                dimg[srng(islot(p, y_), h), :] = acc[pl.ds(o, sizes[h]), :].astype(BF16)
                o += sizes[h]
        if with_rest:
            for h in rest:
                for s in range(n_img):
                    dimg[srng(s, h), :] = acc[pl.ds(o, sizes[h]), :].astype(BF16)
                    o += sizes[h]

    def to_y(e):
        y_ = (ly + e) % n_ly
        image_piece(y_, e == 1)
        for d in [*range(1, n_kl), 0]:
            for h in range(H):
                q = rid["gy"] + d * H + h
                send(dimg.at[srng(islot((kl + d) % n_kl, y_), h), :], ry.at[(e - 1) * n_kl + d, half[h], :],
                     "gy", q, dev(ly_=y_), sizes[h])

    x1 = (lx + 1) % n_lx
    text_piece(order[0], x1, 1 - c, True)
    to_core(order[0], x1, rid["dc"] + n_kh)
    text_piece(order[0], x1, c, True)

    for h in range(H):
        def to_grad(i, _):
            grad_of(span(row0[h] + i * STEP, STEP, STEP), h)
            return 0
        lax.fori_loop(0, height[h] // STEP, to_grad, 0, unroll=2)
    to_x(1, 0)
    for e in range(1, n_ly):
        to_y(e)

    cross = sum(v[4:5] * e for v, e in zip(all_stat, et))
    diverge = cross / tsum - (gt + jnp.log(tsum)) + (gs + jnp.log(ssum))
    part[kh] = jnp.broadcast_to(jnp.sum(diverge, axis=1, keepdims=True), (8, 128))
    for d in range(1, n_kh):
        send(part.at[kh], part.at[kh], "loss", rid["lk"], dev(k_=((kh + d) % n_kh) * n_kl + kl))

    for e in range(1, n_lx):
        x_ = (lx + e) % n_lx
        for i in range(1 if e == 1 else 0, n_kh):
            text_piece(order[i], x_, 1 - c)
            to_core(order[i], x_, rid["dc"] + e * n_kh + i)
            text_piece(order[i], x_, c)
            to_x(e, i)

    got(part.at[pl.ds(0, n_kh - 1)], rid["lk"])
    base = n_kh
    part[base + lx] = sum(part[i] for i in range(n_kh))
    for d in range(1, n_lx):
        send(part.at[base + lx], part.at[base + lx], "loss", rid["lx"], dev(lx_=(lx + d) % n_lx))

    for i in range(n_kh):
        text_piece(order[i], lx, 1 - c)
        to_core(order[i], lx, rid["dc"] + i)
    for i in range(n_kh):
        text_piece(order[i], lx, c)
    image_piece(ly, n_ly == 1)

    got(part.at[pl.ds(0, n_lx - 1)], rid["lx"])
    base = n_kh + n_lx
    part[base + c] = sum(part[n_kh + i] for i in range(n_lx))
    send(part.at[base + c], part.at[base + c], "loss", rid["lc"], dev(c_=1 - c))

    def owner_copy(i, h):
        j = order[i]
        dest = kl * n_kh + j
        op = copy(dtxt.at[srng(tslot(j, lx, c), h), :], r3.at[kh, half[h], :], sid["dz"], rid["dz"], dev(k_=dest))
        return dest, op

    def text_sum(i, h):
        j = order[i]
        s = lx * n_kh + j
        if h == 0:
            got(r1.at[s], rid["dc"] + i)
        rng = srng(tslot(j, lx, c), h)
        v = dtxt[rng, :].astype(F32) + r1[s, half[h], :].astype(F32)
        for e in range(1, n_lx):
            got(r2.at[(e - 1) * n_kh + j, half[h], :], rid["dx"] + (e * n_kh + i) * H + h)
            v = v + r2[(e - 1) * n_kh + j, half[h], :].astype(F32)
        dtxt[rng, :] = v.astype(BF16)
        dest, op = owner_copy(i, h)

        @pl.when(dest != k)
        def _():
            op.start()

        @pl.when(dest == k)
        def _():
            r3[kh, half[h], :] = dtxt[rng, :]

    def got_y(d, h):
        got_rows((n_ly - 1) * sizes[h], rid["gy"] + d * H + h)

    def image_sum(d, h):
        got_y(d, h)
        rng = srng(islot((kl + d) % n_kl, ly), h)
        v = dimg[rng, :].astype(F32)
        for e in range(1, n_ly):
            v = v + ry[(e - 1) * n_kl + d, half[h], :].astype(F32)
        dimg[rng, :] = v.astype(BF16)
        send(dimg.at[rng, :], rz.at[d - 1, half[h], :], "gz", rid["gz"], dev(k_=kh * n_kl + (kl + d) % n_kl), sizes[h])

    for i in range(n_kh):
        for h in range(H):
            text_sum(i, h)
            if 1 <= i + 1 < n_kl:
                image_sum(i + 1, h)
    for d in range(n_kh + 1, n_kl):
        for h in range(H):
            image_sum(d, h)

    got(part.at[base + 1 - c], rid["lc"])
    loss_out[...] = (part[base] + part[base + 1]) / float(D * n_row * n_loop)

    def finish(terms, src, inv_ref, out):
        for o in range(0, D, UNIT):
            rng = pl.ds(o, UNIT)
            g = terms(o)
            x = src[rng, :].astype(F32)
            inv = inv_ref[rng, 0:1]
            along = jnp.sum(g * x, axis=1, keepdims=True) * inv * inv
            out[rng, :] = ((g - x * along) * inv).astype(BF16)

    for h in range(H):
        got_y(0, h)
    got_rows((n_kl - 1) * D, rid["gz"])

    def image_terms(o):
        v = dimg[span(slot0 * D + o, UNIT, UNIT), :].astype(F32)
        for e in range(1, n_ly):
            v = v + ry[(e - 1) * n_kl, pl.ds(o, UNIT), :].astype(F32)
        for d in range(1, n_kl):
            v = v + rz[d - 1, pl.ds(o, UNIT), :].astype(F32)
        return v
    finish(image_terms, si, inv_i, gi_out)

    def on_owner(wait):
        @pl.when(src_kl == kl)
        def _():
            wait(n_kh - 1)

        @pl.when(src_kl != kl)
        def _():
            wait(n_kh)
    on_owner(lambda n: got(txt_s.at[pl.ds(0, n * D), :], rid["dz"]))
    finish(lambda o: sum(r3[g, pl.ds(o, UNIT), :].astype(F32) for g in range(n_kh)), st, inv_t, gt_out)

    for name, raw in (("t_txt", raw_t), ("t_img", raw_i)):
        left(raw.at[pl.ds(0, n_loop - 1)], sid[name])
    left(stat.at[pl.ds(0, n_img - 1)], sid["stat"])
    left_rows("dc", "dx", "gy", "gz")
    left(part.at[pl.ds(0, n_kh - 1 + n_lx - 1 + 1)], sid["loss"])

    on_owner(lambda n: left(txt_s.at[pl.ds(0, n * D), :], sid["dz"]))


def emit(total, gi, gt, loss_out, gi_out, gt_out):
    loss_out[0] = total[0, 0]
    gi_out[...] = gi[...]
    gt_out[...] = gt[...]


def on_device(n_row, n_loop, si, st, ti, tt, ssc, tsc):
    D, code = si.shape
    n_kl, n_lx = 2, 2
    n_kh, n_ly = n_row // (2 * n_kl), n_loop // n_lx
    n_img, n_txt = n_kl * n_ly, n_kh * n_lx * 2
    rows, cols = n_img * D, n_txt * D
    sizes = chunk_sizes(D)
    rid, sid = make_ids(len(sizes), n_kh, n_kl, n_lx, n_ly)
    window = sum(n_kl * s if (n_kl * s) % 128 == 0 else n_img * s for s in sizes)
    dims = (n_row, n_loop, n_kh, n_kl, n_lx, n_ly, D, code)
    vm = pl.BlockSpec(memory_space=pltpu.VMEM)
    sm = pl.BlockSpec(memory_space=pltpu.SMEM)
    V = pltpu.VMEM
    loss, gi, gt = pl.pallas_call(
        functools.partial(kernel, dims, rid, sid),
        out_shape=(
            jax.ShapeDtypeStruct((8, 128), F32),
            jax.ShapeDtypeStruct((D, code), BF16),
            jax.ShapeDtypeStruct((D, code), BF16),
        ),
        in_specs=[vm] * 4 + [sm] * 2,
        out_specs=(vm, vm, vm),
        scratch_shapes=[
            V((rows, code), BF16), V((rows, code), BF16),
            V((D, code), BF16), V((D, code), BF16),
            V((cols, code), BF16), V((cols, code), BF16),
            V((n_loop, D, code // n_loop), BF16), V((n_loop, D, code // n_loop), BF16),
            V((cols, rows), F32), V((cols, rows), F32), V((cols, rows), BF16),
            V((n_img, 8, rows), F32),
            V((window, code), F32),
            V((n_lx * n_kh, D, code), BF16),
            V(((n_lx - 1) * n_kh, D, code), BF16),
            V((n_kh, D, code), BF16),
            V(((n_ly - 1) * n_kl, D, code), BF16),
            V((n_kl - 1, D, code), BF16),
            V((n_kh + n_lx + 2, 8, 128), F32),
            V((D, 128), F32), V((D, 128), F32),
            pltpu.SemaphoreType.DMA((sid.count,)),
            pltpu.SemaphoreType.DMA((rid.count,)),
        ],
        compiler_params=pltpu.CompilerParams(
            collective_id=0, has_side_effects=True, vmem_limit_bytes=67043328,
        ),
    )(si, st, ti, tt, ssc, tsc)
    return pl.pallas_call(
        emit,
        out_shape=(
            jax.ShapeDtypeStruct((1,), F32),
            jax.ShapeDtypeStruct((D, code), BF16),
            jax.ShapeDtypeStruct((D, code), BF16),
        ),
        in_specs=[vm] * 3,
        out_specs=(sm, vm, vm),
    )(loss, gi, gt)


def solution(mesh):
    return jax.shard_map(
        functools.partial(on_device, mesh.shape["row"], mesh.shape["loop"]),
        mesh=mesh,
        in_specs=(
            P(("row", "loop"), None),
            P(("row", "loop"), None),
            P("row", "loop"),
            P("row", "loop"),
            P(),
            P(),
        ),
        out_specs=(P(), P(("row", "loop"), None), P(("row", "loop"), None)),
        check_vma=False,
    )
```

time: 90.8 us -> 99.2 us (1.093)
  the two profiles are of different devices: /device:TPU:21 before, /device:TPU:0 now
where the time goes in v1:
time: 99.2 us; the launch traced here: 99 us
  Pallas kernels  97 us (98%)
  between operations  1.93 us (2%)
    pallas_call x1, Pallas kernels, on_device(): pl.pallas_call(functools.partial(kernel, dims, rid, sid), out_shape=(jax....  95.1 us

profile of v1, /device:TPU:0, one launch (start us, length us, event | category | flops | bytes accessed | tf_op | source)
XLA Modules:
  0.0 99.0 jit_solution(16399656675196603272)
XLA Ops:
  1.9 95.1 %shard_map.85 = (f32[8,128]{1,0:T(8,128)}, bf16[160,1024]{1,0:T(8,128)(2,1)}, bf16[160,1024]{1,0:T(8,128)(2,1)}) custom-call(bf16[160,1024]{1,0:T(8,128)(2,1)} %si.1, bf16[160,1024]{1,0:T(8,128)(2,1)} %st.1, bf16[640,256]{1,0:T(8,128)(2,1)} %ti.1, bf16[640,256]{1,0:T(8,128)(2,1)} %tt.1, f32[1]{0:T(128)S(6)} %copy.9.ssc, f32[1]{0:T(128)S(6)} %copy.10.tsc), custom_call_target="tpu_custom_call" | custom-call | tf_op jit(solution)/shard_map/pallas_call | solution.py:644
  97.0 1.9 %shard_map.86 = (f32[1]{0:T(128)}, bf16[160,1024]{1,0:T(8,128)(2,1)}, bf16[160,1024]{1,0:T(8,128)(2,1)}) custom-call(f32[8,128]{1,0:T(8,128)} %get-tuple-element.6.total, bf16[160,1024]{1,0:T(8,128)(2,1)} %get-tuple-element.7.gi, bf16[160,1024]{1,0:T(8,128)(2,1)} %get-tuple-element.8.gt), custom_call_target="tpu_custom_call" | custom-call | tf_op jit(solution)/shard_map/pallas_call | solution.py:675

commit v2 on v1

--- a/solution.py
+++ b/solution.py
@@ -46,13 +46,12 @@
         recv.take(("tx", a), n_lx * H)
         recv.take(("tc", a), H)
     recv.take("stat")
-    recv.take("dc", n_lx * n_kh)
+    recv.take("dc", n_lx * n_kh * H)
     recv.take("dx", n_lx * n_kh * H)
     recv.take("dz")
     recv.take("gy", n_kl * H)
     recv.take("gz")
-    for name in ("lk", "lx", "lc"):
-        recv.take(name)
+    recv.take("loss")
     for name in ("t_img", "t_txt", "stat", "dc", "dx", "dz", "gy", "gz", "loss"):
         sent.take(name)
     for a in range(2):
@@ -141,8 +140,19 @@
         for name in names:
             left(txt_s.at[pl.ds(0, sent_rows.pop(name)), :], sid[name])
 
+    loss_peers = [
+        (kd, xd, cd) for kd in range(n_kh) for xd in range(n_lx) for cd in range(2) if kd or xd or cd
+    ]
+
+    def loss_peer(kd, xd, cd):
+        return dev(k_=((kh + kd) % n_kh) * n_kl + kl, c_=(c + cd) % 2, lx_=(lx + xd) % n_lx)
+
     barrier = pltpu.get_barrier_semaphore()
     n_peer = 0
+    for kd, xd, cd in loss_peers:
+        if (kd != 0) + (xd != 0) + (cd != 0) > 1:
+            pl.semaphore_signal(barrier, inc=1, device_id=loss_peer(kd, xd, cd), device_id_type=MESH)
+            n_peer += 1
     for d in range(1, n_loop):
         pl.semaphore_signal(barrier, inc=1, device_id=(r, (l + d) % n_loop), device_id_type=MESH)
         n_peer += 1
@@ -196,6 +206,9 @@
         for d in range(1, n_kl):
             q = rid[("iz", a)] + d * H + h
             send(buf.at[rng, :], buf.at[rng, :], ("img", a), q, dev(k_=kh * n_kl + (kl + d) % n_kl), sizes[h])
+
+    def image_y(a, buf, h):
+        rng = irng(h, slot0)
         for e in range(1, n_ly):
             send(buf.at[rng, :], buf.at[rng, :], ("img", a), rid[("iy", a)] + h, dev(ly_=(ly + e) % n_ly), sizes[h])
 
@@ -275,6 +288,7 @@
         if h:
             own_image(h)
         image_first(0, img_s, h)
+        image_y(0, img_s, h)
     text_relay(0, txt_s, 0)
     image_relay(0, img_s, 0)
     teacher_wait(tt, raw_t, "t_txt")
@@ -289,8 +303,10 @@
         text_relay(0, txt_s, h)
         image_relay(0, img_s, h)
     for h in range(H):
+        image_y(1, img_t, h)
+    for h in range(H):
         text_cross(0, txt_s, h)
-        if h == 0:
+        if h == H - 2:
             text_relay(1, txt_t, 0)
             image_relay(1, img_t, 0)
     for h in range(H):
@@ -361,9 +377,7 @@
     for h in range(1, H):
         text_relay(1, txt_t, h)
         image_relay(1, img_t, h)
-        if h < H - 1:
-            arrive(h - 1)
-    for h in range(max(H - 2, 0), H):
+    for h in range(H):
         arrive(h)
 
     best = [functools.reduce(jnp.maximum, [tops[h, hi] for h in range(hi, H)]) for hi in range(H)]
@@ -396,6 +410,13 @@
     et = [jnp.exp(v[1:2] - gt) for v in all_stat]
     ssum = sum(v[2:3] * e for v, e in zip(all_stat, es))
     tsum = sum(v[3:4] * e for v, e in zip(all_stat, et))
+    cross = sum(v[4:5] * e for v, e in zip(all_stat, et))
+    diverge = cross / tsum - (gt + jnp.log(tsum)) + (gs + jnp.log(ssum))
+    mine = tslot(kh, lx, c)
+    part[mine] = jnp.broadcast_to(jnp.sum(diverge, axis=1, keepdims=True), (8, 128))
+    for peer in loss_peers:
+        send(part.at[mine], part.at[mine], "loss", rid["loss"], loss_peer(*peer))
+
     s_mul = sscale * jnp.exp(smax - gs) / ssum
     t_scale = sscale / tsum
 
@@ -420,19 +441,27 @@
         v = jnp.dot(jnp.concatenate(g, axis=0), img_s[...], preferred_element_type=F32)
         dtxt[at(slot), :] = v.astype(BF16)
 
-    def to_core(j, x_, q):
-        send(dtxt.at[at(tslot(j, x_, 1 - c)), :], r1.at[x_ * n_kh + j], "dc", q, dev(c_=1 - c), D)
-
     order = [(n_kh - 1 - kh + i) % n_kh for i in range(n_kh)]
+
+    def to_core(e, i, fresh=False):
+        x_ = (lx + e) % n_lx
+        j = order[i]
+        text_piece(j, x_, 1 - c, fresh)
+        for h in range(H):
+            send(dtxt.at[srng(tslot(j, x_, 1 - c), h), :], r1.at[x_ * n_kh + j, half[h], :], "dc",
+                 rid["dc"] + (e * n_kh + i) * H + h, dev(c_=1 - c), sizes[h])
+
+    def from_core(e, i, h):
+        s = ((lx + e) % n_lx) * n_kh + order[i]
+        got(r1.at[s, half[h], :], rid["dc"] + (e * n_kh + i) * H + h)
+        return r1[s, half[h], :].astype(F32)
 
     def to_x(e, i):
         x_ = (lx + e) % n_lx
         j = order[i]
-        s = x_ * n_kh + j
-        got(r1.at[s], rid["dc"] + e * n_kh + i)
         for h in range(H):
             rng = srng(tslot(j, x_, c), h)
-            dtxt[rng, :] = (dtxt[rng, :].astype(F32) + r1[s, half[h], :].astype(F32)).astype(BF16)
+            dtxt[rng, :] = (dtxt[rng, :].astype(F32) + from_core(e, i, h)).astype(BF16)
             q = rid["dx"] + (e * n_kh + i) * H + h
             send(dtxt.at[rng, :], r2.at[(e - 1) * n_kh + j, half[h], :], "dx", q, dev(lx_=x_), sizes[h])
 
@@ -484,10 +513,8 @@
                      "gy", q, dev(ly_=y_), sizes[h])
 
     x1 = (lx + 1) % n_lx
-    text_piece(order[0], x1, 1 - c, True)
-    to_core(order[0], x1, rid["dc"] + n_kh)
+    to_core(1, 0, True)
     text_piece(order[0], x1, c, True)
-
     for h in range(H):
         def to_grad(i, _):
             grad_of(span(row0[h] + i * STEP, STEP, STEP), h)
@@ -496,38 +523,17 @@
     to_x(1, 0)
     for e in range(1, n_ly):
         to_y(e)
-
-    cross = sum(v[4:5] * e for v, e in zip(all_stat, et))
-    diverge = cross / tsum - (gt + jnp.log(tsum)) + (gs + jnp.log(ssum))
-    part[kh] = jnp.broadcast_to(jnp.sum(diverge, axis=1, keepdims=True), (8, 128))
-    for d in range(1, n_kh):
-        send(part.at[kh], part.at[kh], "loss", rid["lk"], dev(k_=((kh + d) % n_kh) * n_kl + kl))
-
+    to_core(0, 0)
+    text_piece(order[0], lx, c)
     for e in range(1, n_lx):
-        x_ = (lx + e) % n_lx
         for i in range(1 if e == 1 else 0, n_kh):
-            text_piece(order[i], x_, 1 - c)
-            to_core(order[i], x_, rid["dc"] + e * n_kh + i)
-            text_piece(order[i], x_, c)
-            to_x(e, i)
-
-    got(part.at[pl.ds(0, n_kh - 1)], rid["lk"])
-    base = n_kh
-    part[base + lx] = sum(part[i] for i in range(n_kh))
-    for d in range(1, n_lx):
-        send(part.at[base + lx], part.at[base + lx], "loss", rid["lx"], dev(lx_=(lx + d) % n_lx))
-
-    for i in range(n_kh):
-        text_piece(order[i], lx, 1 - c)
-        to_core(order[i], lx, rid["dc"] + i)
-    for i in range(n_kh):
-        text_piece(order[i], lx, c)
+            to_core(e, i)
+            text_piece(order[i], (lx + e) % n_lx, c)
+            if e > 1 or i > 1:
+                to_x(e, i)
     image_piece(ly, n_ly == 1)
-
-    got(part.at[pl.ds(0, n_lx - 1)], rid["lx"])
-    base = n_kh + n_lx
-    part[base + c] = sum(part[n_kh + i] for i in range(n_lx))
-    send(part.at[base + c], part.at[base + c], "loss", rid["lc"], dev(c_=1 - c))
+    if n_kh > 1:
+        to_x(1, 1)
 
     def owner_copy(i, h):
         j = order[i]
@@ -537,11 +543,8 @@
 
     def text_sum(i, h):
         j = order[i]
-        s = lx * n_kh + j
-        if h == 0:
-            got(r1.at[s], rid["dc"] + i)
         rng = srng(tslot(j, lx, c), h)
-        v = dtxt[rng, :].astype(F32) + r1[s, half[h], :].astype(F32)
+        v = dtxt[rng, :].astype(F32) + from_core(0, i, h)
         for e in range(1, n_lx):
             got(r2.at[(e - 1) * n_kh + j, half[h], :], rid["dx"] + (e * n_kh + i) * H + h)
             v = v + r2[(e - 1) * n_kh + j, half[h], :].astype(F32)
@@ -571,14 +574,16 @@
     for i in range(n_kh):
         for h in range(H):
             text_sum(i, h)
+            if h == 0 and i + 1 < n_kh:
+                to_core(0, i + 1)
+                text_piece(order[i + 1], lx, c)
             if 1 <= i + 1 < n_kl:
                 image_sum(i + 1, h)
     for d in range(n_kh + 1, n_kl):
         for h in range(H):
             image_sum(d, h)
-
-    got(part.at[base + 1 - c], rid["lc"])
-    loss_out[...] = (part[base] + part[base + 1]) / float(D * n_row * n_loop)
+    got(part.at[pl.ds(0, len(loss_peers))], rid["loss"])
+    loss_out[...] = sum(part[i] for i in range(n_txt)) / float(D * n_row * n_loop)
 
     def finish(terms, src, inv_ref, out):
         for o in range(0, D, UNIT):
@@ -617,7 +622,7 @@
         left(raw.at[pl.ds(0, n_loop - 1)], sid[name])
     left(stat.at[pl.ds(0, n_img - 1)], sid["stat"])
     left_rows("dc", "dx", "gy", "gz")
-    left(part.at[pl.ds(0, n_kh - 1 + n_lx - 1 + 1)], sid["loss"])
+    left(part.at[pl.ds(0, len(loss_peers))], sid["loss"])
 
     on_owner(lambda n: left(txt_s.at[pl.ds(0, n * D), :], sid["dz"]))
 
@@ -663,7 +668,7 @@
             V((n_kh, D, code), BF16),
             V(((n_ly - 1) * n_kl, D, code), BF16),
             V((n_kl - 1, D, code), BF16),
-            V((n_kh + n_lx + 2, 8, 128), F32),
+            V((n_txt, 8, 128), F32),
             V((D, 128), F32), V((D, 128), F32),
             pltpu.SemaphoreType.DMA((sid.count,)),
             pltpu.SemaphoreType.DMA((rid.count,)),

time: 99.2 us -> 84.6 us (0.85)
  Pallas kernels: 97 us -> 82.5 us
    pallas_call x1, Pallas kernels: 95.1 us -> 80.6 us  [on_device(): pl.pallas_call(functools.partial(kernel, dims, rid, sid), out_shape=(jax....]
where the time goes in v2:
time: 84.6 us; the launch traced here: 84.5 us
  Pallas kernels  82.5 us (98%)
  between operations  1.93 us (2%)
    pallas_call x1, Pallas kernels, on_device(): pl.pallas_call(functools.partial(kernel, dims, rid, sid), out_shape=(jax....  80.6 us
    pallas_call x1, Pallas kernels, on_device(): pl.pallas_call(emit, out_shape=(jax.ShapeDtypeStruct((1,), F32), jax.Shap...  1.94 us

profile of v2, /device:TPU:0, one launch (start us, length us, event | category | flops | bytes accessed | tf_op | source)
XLA Modules:
  0.0 84.5 jit_solution(17067649886544774623)
XLA Ops:
  1.9 80.6 %shard_map.85 = (f32[8,128]{1,0:T(8,128)}, bf16[160,1024]{1,0:T(8,128)(2,1)}, bf16[160,1024]{1,0:T(8,128)(2,1)}) custom-call(bf16[160,1024]{1,0:T(8,128)(2,1)} %si.1, bf16[160,1024]{1,0:T(8,128)(2,1)} %st.1, bf16[640,256]{1,0:T(8,128)(2,1)} %ti.1, bf16[640,256]{1,0:T(8,128)(2,1)} %tt.1, f32[1]{0:T(128)S(6)} %copy.9.ssc, f32[1]{0:T(128)S(6)} %copy.10.tsc), custom_call_target="tpu_custom_call" | custom-call | tf_op jit(solution)/shard_map/pallas_call | solution.py:649
  82.5 1.9 %shard_map.86 = (f32[1]{0:T(128)}, bf16[160,1024]{1,0:T(8,128)(2,1)}, bf16[160,1024]{1,0:T(8,128)(2,1)}) custom-call(f32[8,128]{1,0:T(8,128)} %get-tuple-element.6.total, bf16[160,1024]{1,0:T(8,128)(2,1)} %get-tuple-element.7.gi, bf16[160,1024]{1,0:T(8,128)(2,1)} %get-tuple-element.8.gt), custom_call_target="tpu_custom_call" | custom-call | tf_op jit(solution)/shard_map/pallas_call | solution.py:680

commit v3 on v2

--- a/solution.py
+++ b/solution.py
@@ -13,6 +13,7 @@
 PART = 64
 UNIT = 32
 STEP = 32
+DOT = 1280
 
 
 class Ids:
@@ -65,7 +66,7 @@
     si, st, ti, tt, ssc, tsc,
     loss_out, gi_out, gt_out,
     img_s, img_t, own_s, own_t, txt_s, txt_t, raw_i, raw_t,
-    slog, tlog, grad, stat, acc, r1, r2, r3, ry, rz, part, inv_i, inv_t,
+    slog, tlog, grad, stat, r1, r2, r3, ry, rz, part, inv_i, inv_t,
     ss, rs,
 ):
     n_row, n_loop, n_kh, n_kl, n_lx, n_ly, D, code = dims
@@ -114,6 +115,7 @@
         return span(slot * D, D, UNIT)
 
     half = [pl.ds(off[h], sizes[h]) for h in range(H)]
+    back = sorted(range(H), key=lambda h: sizes[h])
 
     def copy(src, dst, q_send, q_recv, device):
         return pltpu.make_async_remote_copy(
@@ -313,20 +315,21 @@
         image_finish(0, h)
         text_finish(0, h)
 
-    TILE = 256
+    def tile_of(n):
+        return max(t for t in range(UNIT, min(n, DOT) + 1, UNIT) if n % t == 0)
 
     def logits(txt, img, scale, out, row0, n, lane0, width):
         lanes = pl.ds(lane0, width)
 
-        def body(i, m):
-            o = pl.multiple_of(row0 + i * TILE, TILE)
+        tile = tile_of(n)
+        m = jnp.full((8, width), -jnp.inf, F32)
+        for o in range(row0, row0 + n, tile):
             v = scale * lax.dot_general(
-                txt[pl.ds(o, TILE), :], img[lanes, :], (((1,), (1,)), ((), ())),
+                txt[pl.ds(o, tile), :], img[lanes, :], (((1,), (1,)), ((), ())),
                 preferred_element_type=F32,
             )
-            out[pl.ds(o, TILE), lanes] = v
-            return jnp.maximum(m, jnp.max(v.reshape(TILE // 8, 8, width), axis=0))
-        m = lax.fori_loop(0, n // TILE, body, jnp.full((8, width), -jnp.inf, F32))
+            out[pl.ds(o, tile), lanes] = v
+            m = jnp.maximum(m, jnp.max(v.reshape(tile // 8, 8, width), axis=0))
         return jnp.max(m, axis=0, keepdims=True)
 
     smax = logits(txt_s, img_s, sscale, slog, 0, cols, 0, rows)
@@ -367,17 +370,20 @@
         sums[h, hi] = exps(first, n, lane0[hi], width[hi], m)
 
     def arrive(h):
-        text_cross(1, txt_t, h)
         image_finish(1, h)
         text_finish(1, h)
         for hi in range(h):
             group(h, hi)
+        if 0 < h < H - 1:
+            text_cross(1, txt_t, h + 1)
         group(h, h)
 
     for h in range(1, H):
         text_relay(1, txt_t, h)
         image_relay(1, img_t, h)
     for h in range(H):
+        if h < 2:
+            text_cross(1, txt_t, h)
         arrive(h)
 
     best = [functools.reduce(jnp.maximum, [tops[h, hi] for h in range(hi, H)]) for hi in range(H)]
@@ -447,7 +453,7 @@
         x_ = (lx + e) % n_lx
         j = order[i]
         text_piece(j, x_, 1 - c, fresh)
-        for h in range(H):
+        for h in back:
             send(dtxt.at[srng(tslot(j, x_, 1 - c), h), :], r1.at[x_ * n_kh + j, half[h], :], "dc",
                  rid["dc"] + (e * n_kh + i) * H + h, dev(c_=1 - c), sizes[h])
 
@@ -459,7 +465,7 @@
     def to_x(e, i):
         x_ = (lx + e) % n_lx
         j = order[i]
-        for h in range(H):
+        for h in back:
             rng = srng(tslot(j, x_, c), h)
             dtxt[rng, :] = (dtxt[rng, :].astype(F32) + from_core(e, i, h)).astype(BF16)
             q = rid["dx"] + (e * n_kh + i) * H + h
@@ -468,46 +474,33 @@
     dimg = img_t
     full = [h for h in range(H) if (n_kl * sizes[h]) % 128 == 0]
     rest = [h for h in range(H) if h not in full]
-    KT = 256
 
     def image_piece(y_, with_rest):
         windows = [pl.ds(pl.multiple_of(lane0[h] + y_ * n_kl * sizes[h], 128), n_kl * sizes[h]) for h in full]
-        lens = [n_kl * sizes[h] for h in full]
         if with_rest:
             windows += [pl.ds(lane0[h], width[h]) for h in rest]
-            lens += [width[h] for h in rest]
-        M = sum(lens)
-
-        def body(i, _):
-            o = pl.multiple_of(i * KT, KT)
-            g = jnp.concatenate([grad[pl.ds(o, KT), w] for w in windows], axis=1)
-            v = lax.dot_general(g, txt_s[pl.ds(o, KT), :], (((0,), (0,)), ((), ())), preferred_element_type=F32)
-
-            @pl.when(i == 0)
-            def _():
-                acc[pl.ds(0, M), :] = v
-
-            @pl.when(i != 0)
-            def _():
-                acc[pl.ds(0, M), :] += v
-            return 0
-        lax.fori_loop(0, cols // KT, body, 0)
+        tile = tile_of(cols)
+        v = 0.0
+        for o in range(0, cols, tile):
+            g = jnp.concatenate([grad[pl.ds(o, tile), w] for w in windows], axis=1)
+            v = v + lax.dot_general(g, txt_s[pl.ds(o, tile), :], (((0,), (0,)), ((), ())), preferred_element_type=F32)
+        v = v.astype(BF16)
         o = 0
         for h in full:
             for p in range(n_kl):
-                dimg[srng(islot(p, y_), h), :] = acc[pl.ds(o, sizes[h]), :].astype(BF16)
+                dimg[srng(islot(p, y_), h), :] = v[o:o + sizes[h]]
                 o += sizes[h]
         if with_rest:
             for h in rest:
                 for s in range(n_img):
-                    dimg[srng(s, h), :] = acc[pl.ds(o, sizes[h]), :].astype(BF16)
+                    dimg[srng(s, h), :] = v[o:o + sizes[h]]
                     o += sizes[h]
 
     def to_y(e):
         y_ = (ly + e) % n_ly
         image_piece(y_, e == 1)
         for d in [*range(1, n_kl), 0]:
-            for h in range(H):
+            for h in back:
                 q = rid["gy"] + d * H + h
                 send(dimg.at[srng(islot((kl + d) % n_kl, y_), h), :], ry.at[(e - 1) * n_kl + d, half[h], :],
                      "gy", q, dev(ly_=y_), sizes[h])
@@ -521,10 +514,48 @@
             return 0
         lax.fori_loop(0, height[h] // STEP, to_grad, 0, unroll=2)
     to_x(1, 0)
+    to_core(0, 0)
+    text_piece(order[0], lx, c)
     for e in range(1, n_ly):
         to_y(e)
-    to_core(0, 0)
-    text_piece(order[0], lx, c)
+
+    def owner_copy(i, h):
+        j = order[i]
+        dest = kl * n_kh + j
+        op = copy(dtxt.at[srng(tslot(j, lx, c), h), :], r3.at[kh, half[h], :], sid["dz"], rid["dz"], dev(k_=dest))
+        return dest, op
+
+    def text_sum(i, h):
+        j = order[i]
+        rng = srng(tslot(j, lx, c), h)
+        v = dtxt[rng, :].astype(F32) + from_core(0, i, h)
+        for e in range(1, n_lx):
+            got(r2.at[(e - 1) * n_kh + j, half[h], :], rid["dx"] + (e * n_kh + i) * H + h)
+            v = v + r2[(e - 1) * n_kh + j, half[h], :].astype(F32)
+        dtxt[rng, :] = v.astype(BF16)
+        dest, op = owner_copy(i, h)
+
+        @pl.when(dest != k)
+        def _():
+            op.start()
+
+        @pl.when(dest == k)
+        def _():
+            r3[kh, half[h], :] = dtxt[rng, :]
+
+    def got_y(d, h):
+        got_rows((n_ly - 1) * sizes[h], rid["gy"] + d * H + h)
+
+    def image_sum(d, h):
+        got_y(d, h)
+        rng = srng(islot((kl + d) % n_kl, ly), h)
+        v = dimg[rng, :].astype(F32)
+        for e in range(1, n_ly):
+            v = v + ry[(e - 1) * n_kl + d, half[h], :].astype(F32)
+        dimg[rng, :] = v.astype(BF16)
+        send(dimg.at[rng, :], rz.at[d - 1, half[h], :], "gz", rid["gz"], dev(k_=kh * n_kl + (kl + d) % n_kl), sizes[h])
+
+    text_sum(0, back[0])
     for e in range(1, n_lx):
         for i in range(1 if e == 1 else 0, n_kh):
             to_core(e, i)
@@ -534,54 +565,17 @@
     image_piece(ly, n_ly == 1)
     if n_kh > 1:
         to_x(1, 1)
-
-    def owner_copy(i, h):
-        j = order[i]
-        dest = kl * n_kh + j
-        op = copy(dtxt.at[srng(tslot(j, lx, c), h), :], r3.at[kh, half[h], :], sid["dz"], rid["dz"], dev(k_=dest))
-        return dest, op
-
-    def text_sum(i, h):
-        j = order[i]
-        rng = srng(tslot(j, lx, c), h)
-        v = dtxt[rng, :].astype(F32) + from_core(0, i, h)
-        for e in range(1, n_lx):
-            got(r2.at[(e - 1) * n_kh + j, half[h], :], rid["dx"] + (e * n_kh + i) * H + h)
-            v = v + r2[(e - 1) * n_kh + j, half[h], :].astype(F32)
-        dtxt[rng, :] = v.astype(BF16)
-        dest, op = owner_copy(i, h)
-
-        @pl.when(dest != k)
-        def _():
-            op.start()
-
-        @pl.when(dest == k)
-        def _():
-            r3[kh, half[h], :] = dtxt[rng, :]
-
-    def got_y(d, h):
-        got_rows((n_ly - 1) * sizes[h], rid["gy"] + d * H + h)
-
-    def image_sum(d, h):
-        got_y(d, h)
-        rng = srng(islot((kl + d) % n_kl, ly), h)
-        v = dimg[rng, :].astype(F32)
-        for e in range(1, n_ly):
-            v = v + ry[(e - 1) * n_kl + d, half[h], :].astype(F32)
-        dimg[rng, :] = v.astype(BF16)
-        send(dimg.at[rng, :], rz.at[d - 1, half[h], :], "gz", rid["gz"], dev(k_=kh * n_kl + (kl + d) % n_kl), sizes[h])
-
-    for i in range(n_kh):
-        for h in range(H):
-            text_sum(i, h)
-            if h == 0 and i + 1 < n_kh:
+    texts = [(i, h) for i in range(n_kh) for h in back][1:]
+    images = [(d, h) for d in range(1, n_kl) for h in back]
+    while texts or images:
+        if texts:
+            i, h = texts.pop(0)
+            if h == back[-1] and i + 1 < n_kh:
                 to_core(0, i + 1)
                 text_piece(order[i + 1], lx, c)
-            if 1 <= i + 1 < n_kl:
-                image_sum(i + 1, h)
-    for d in range(n_kh + 1, n_kl):
-        for h in range(H):
-            image_sum(d, h)
+            text_sum(i, h)
+        if images:
+            image_sum(*images.pop(0))
     got(part.at[pl.ds(0, len(loss_peers))], rid["loss"])
     loss_out[...] = sum(part[i] for i in range(n_txt)) / float(D * n_row * n_loop)
 
@@ -641,7 +635,6 @@
     rows, cols = n_img * D, n_txt * D
     sizes = chunk_sizes(D)
     rid, sid = make_ids(len(sizes), n_kh, n_kl, n_lx, n_ly)
-    window = sum(n_kl * s if (n_kl * s) % 128 == 0 else n_img * s for s in sizes)
     dims = (n_row, n_loop, n_kh, n_kl, n_lx, n_ly, D, code)
     vm = pl.BlockSpec(memory_space=pltpu.VMEM)
     sm = pl.BlockSpec(memory_space=pltpu.SMEM)
@@ -662,7 +655,6 @@
             V((n_loop, D, code // n_loop), BF16), V((n_loop, D, code // n_loop), BF16),
             V((cols, rows), F32), V((cols, rows), F32), V((cols, rows), BF16),
             V((n_img, 8, rows), F32),
-            V((window, code), F32),
             V((n_lx * n_kh, D, code), BF16),
             V(((n_lx - 1) * n_kh, D, code), BF16),
             V((n_kh, D, code), BF16),

time: 84.6 us -> 82.1 us (0.970)
  Pallas kernels: 82.5 us -> 79.9 us
    pallas_call x1, Pallas kernels: 80.6 us -> 78 us  [on_device(): pl.pallas_call(functools.partial(kernel, dims, rid, sid), out_shape=(jax....]
where the time goes in v3:
time: 82.1 us; the launch traced here: 81.9 us
  Pallas kernels  79.9 us (97%)
  between operations  1.93 us (2%)
    pallas_call x1, Pallas kernels, on_device(): pl.pallas_call(functools.partial(kernel, dims, rid, sid), out_shape=(jax....  78 us
    pallas_call x1, Pallas kernels, on_device(): pl.pallas_call(emit, out_shape=(jax.ShapeDtypeStruct((1,), F32), jax.Shap...  1.94 us

profile of v3, /device:TPU:0, one launch (start us, length us, event | category | flops | bytes accessed | tf_op | source)
XLA Modules:
  0.0 81.9 jit_solution(11849036729178135091)
XLA Ops:
  1.9 78.0 %shard_map.85 = (f32[8,128]{1,0:T(8,128)}, bf16[160,1024]{1,0:T(8,128)(2,1)}, bf16[160,1024]{1,0:T(8,128)(2,1)}) custom-call(bf16[160,1024]{1,0:T(8,128)(2,1)} %si.1, bf16[160,1024]{1,0:T(8,128)(2,1)} %st.1, bf16[640,256]{1,0:T(8,128)(2,1)} %ti.1, bf16[640,256]{1,0:T(8,128)(2,1)} %tt.1, f32[1]{0:T(128)S(6)} %copy.9.ssc, f32[1]{0:T(128)S(6)} %copy.10.tsc), custom_call_target="tpu_custom_call" | custom-call | tf_op jit(solution)/shard_map/pallas_call | solution.py:642
  79.9 1.9 %shard_map.86 = (f32[1]{0:T(128)}, bf16[160,1024]{1,0:T(8,128)(2,1)}, bf16[160,1024]{1,0:T(8,128)(2,1)}) custom-call(f32[8,128]{1,0:T(8,128)} %get-tuple-element.6.total, bf16[160,1024]{1,0:T(8,128)(2,1)} %get-tuple-element.7.gi, bf16[160,1024]{1,0:T(8,128)(2,1)} %get-tuple-element.8.gt), custom_call_target="tpu_custom_call" | custom-call | tf_op jit(solution)/shard_map/pallas_call | solution.py:672

commit v4 on v3

v4 whole, which is shorter than its diff:
```python
import functools
import jax
import jax.numpy as jnp
from jax import lax
from jax.experimental import pallas as pl
from jax.experimental.pallas import tpu as pltpu
from jax.sharding import PartitionSpec as P

EPS = 1e-06
F32 = jnp.float32
BF16 = jnp.bfloat16
MESH = pl.DeviceIdType.MESH
UNIT = 32
IMAGE_PART = 64
STEP = 32
DOT = 1280
TILE = 256


class Ids:
    def __init__(self):
        self.table = {}
        self.count = 0

    def take(self, name, size=1):
        self.table[name] = self.count
        self.count += size

    def __getitem__(self, name):
        return self.table[name]


def split(D, part):
    return [min(part, D - o) for o in range(0, D, part)]


def offsets(sizes):
    return [sum(sizes[:h]) for h in range(len(sizes))]


def back_sizes(D):
    units = D // UNIT
    if units < 4:
        return [UNIT] * units
    return [UNIT, D - 3 * UNIT, UNIT, UNIT]


def make_ids(D, n_kh, n_kl, n_lx, n_ly):
    HI, HT, HB = len(split(D, IMAGE_PART)), D // UNIT, len(back_sizes(D))
    recv, sent = Ids(), Ids()
    recv.take("t_img")
    recv.take("t_txt")
    for a in range(2):
        recv.take(("iz", a), n_kl * HI)
        recv.take(("iy", a), HI)
        recv.take(("tz", a), n_kh * HT)
        recv.take(("tx", a), n_lx * HT)
        recv.take(("tc", a), HT)
    recv.take("stat")
    recv.take("dc", n_lx * n_kh * HB)
    recv.take("dx", n_lx * n_kh * HB)
    recv.take("dz")
    recv.take("gy", n_kl * HB)
    recv.take("gz")
    recv.take("loss")
    recv.take("keep")
    for name in ("t_img", "t_txt", "stat", "dc", "dx", "dz", "gy", "gz", "loss"):
        sent.take(name)
    for a in range(2):
        for kind in ("img", "first", "txt"):
            sent.take((kind, a))
    return recv, sent


def kernel(
    dims, rid, sid,
    si, st, ti, tt, ssc, tsc,
    loss_out, gi_out, gt_out,
    img_s, img_t, own_s, own_t, txt_s, txt_t, raw_i, raw_t,
    slog, tlog, grad, stat, r1, r2, r3, ry, rz, part, inv_i, inv_t,
    ss, rs,
):
    n_row, n_loop, n_kh, n_kl, n_lx, n_ly, D, code = dims
    isz, tsz, bsz = split(D, IMAGE_PART), split(D, UNIT), back_sizes(D)
    ioff, toff, boff = offsets(isz), offsets(tsz), offsets(bsz)
    HI, HT, HB = len(isz), len(tsz), len(bsz)
    n_img = n_kl * n_ly
    n_txt = n_kh * n_lx * 2
    rows = n_img * D
    cols = n_txt * D
    r = lax.axis_index("row")
    l = lax.axis_index("loop")
    k, c = r // 2, r % 2
    kh, kl = k // n_kl, k % n_kl
    src_kl, src_j = k // n_kh, k % n_kh
    ly, lx = l // n_lx, l % n_lx
    sscale = ssc[0]
    tscale = tsc[0]

    def dev(k_=None, c_=None, ly_=None, lx_=None):
        kk = k if k_ is None else k_
        cc = c if c_ is None else c_
        yy = ly if ly_ is None else ly_
        xx = lx if lx_ is None else lx_
        return (kk * 2 + cc, yy * n_lx + xx)

    def islot(kl_, ly_):
        return ly_ * n_kl + kl_

    def tslot(j, lx_, c_):
        return (j * n_lx + lx_) * 2 + c_

    def span(start, size, step):
        return pl.ds(pl.multiple_of(start, step), size)

    def irng(h, slot):
        return span(n_img * ioff[h] + slot * isz[h], isz[h], UNIT)

    def trng(h, slot):
        return span(n_txt * toff[h] + slot * tsz[h], tsz[h], UNIT)

    def brng(slot, h):
        return span(slot * D + boff[h], bsz[h], UNIT)

    def at(slot):
        return span(slot * D, D, UNIT)

    part_of = [pl.ds(boff[h], bsz[h]) for h in range(HB)]

    def image_ref(a, kl_, ly_, h):
        if a == 0:
            return img_s.at[irng(h, islot(kl_, ly_)), :]
        return raw_i.at[kl_, ly_, :, pl.ds(n_ly * ioff[h], n_ly * isz[h]), :]

    def text_ref(a, j, lx_, h):
        if a == 0:
            return txt_s.at[trng(h, tslot(j, lx_, c)), :]
        return raw_t.at[j, lx_, :, pl.ds(n_lx * toff[h], n_lx * tsz[h]), :]

    def own_ref(a, h):
        if a == 0:
            return own_s.at[pl.ds(toff[h], tsz[h]), :]
        return own_t.at[:, pl.ds(n_lx * toff[h], n_lx * tsz[h]), :]

    def copy(src, dst, q_send, q_recv, device):
        return pltpu.make_async_remote_copy(
            src_ref=src, dst_ref=dst, send_sem=ss.at[q_send], recv_sem=rs.at[q_recv],
            device_id=device, device_id_type=MESH,
        )

    sent_rows = {}

    def send(src, dst, name, q, device, n=0):
        copy(src, dst, sid[name], q, device).start()
        sent_rows[name] = sent_rows.get(name, 0) + n

    def got(dst, q):
        copy(dst, dst, 0, q, dev(c_=1 - c)).wait_recv()

    def got_rows(n, q):
        got(txt_s.at[pl.ds(0, n), :], q)

    def left(ref, q):
        copy(ref, ref, q, 0, dev(c_=1 - c)).wait_send()

    def left_rows(*names):
        for name in names:
            left(txt_s.at[pl.ds(0, sent_rows.pop(name)), :], sid[name])

    loss_peers = [
        (kd, xd, cd) for kd in range(n_kh) for xd in range(n_lx) for cd in range(2) if kd or xd or cd
    ]

    def loss_peer(kd, xd, cd):
        return dev(k_=((kh + kd) % n_kh) * n_kl + kl, c_=(c + cd) % 2, lx_=(lx + xd) % n_lx)

    barrier = pltpu.get_barrier_semaphore()
    n_peer = 0
    for kd, xd, cd in loss_peers:
        if (kd != 0) + (xd != 0) + (cd != 0) > 1:
            pl.semaphore_signal(barrier, inc=1, device_id=loss_peer(kd, xd, cd), device_id_type=MESH)
            n_peer += 1
    for e in range(1, n_ly):
        pl.semaphore_signal(barrier, inc=1, device_id=dev(ly_=(ly + e) % n_ly), device_id_type=MESH)
        n_peer += 1
    for e in range(1, n_lx):
        pl.semaphore_signal(barrier, inc=1, device_id=dev(lx_=(lx + e) % n_lx), device_id_type=MESH)
        n_peer += 1
    for d in range(1, n_kh * n_kl):
        pl.semaphore_signal(barrier, inc=1, device_id=dev(k_=(k + d) % (n_kh * n_kl)), device_id_type=MESH)
        n_peer += 1
    pl.semaphore_signal(barrier, inc=1, device_id=dev(c_=1 - c), device_id_type=MESH)
    n_peer += 1
    for d in range(1, n_kl):
        for e in range(1, n_ly):
            diagonal = dev(k_=kh * n_kl + (kl + d) % n_kl, ly_=(ly + e) % n_ly)
            pl.semaphore_signal(barrier, inc=1, device_id=diagonal, device_id_type=MESH)
            n_peer += 1

    def unit(load, dst, first, n, keep=None):
        for o in range(0, n, UNIT):
            x = load(o)
            n2 = jnp.sum(x * x, axis=1, keepdims=True) + EPS
            inv = 1.0 / jnp.sqrt(n2)
            if keep is not None:
                keep(o, inv)
            dst[span(first + o, UNIT, UNIT), :] = (x * inv).astype(BF16)

    def student_unit(src, dst, first, o0, n, inv_ref):
        def load(o):
            return src[pl.ds(o0 + o, UNIT), :].astype(F32)

        def keep(o, inv):
            inv_ref[pl.ds(o0 + o, UNIT), :] = jnp.broadcast_to(inv, (UNIT, 128))
        unit(load, dst, first, n, keep)

    def own_text(h):
        student_unit(st, own_s, toff[h], toff[h], tsz[h], inv_t)

    def own_image(h):
        student_unit(si, img_s, n_img * ioff[h] + islot(kl, ly) * isz[h], ioff[h], isz[h], inv_i)

    def teacher_keep():
        for h in range(HI):
            for y_ in range(n_ly):
                dst = pl.ds(n_ly * ioff[h] + y_ * isz[h], isz[h])
                src = span((y_ * n_lx + lx) * D + ioff[h], isz[h], UNIT)
                pltpu.make_async_copy(ti.at[src, :], raw_i.at[kl, ly, lx, dst, :], rs.at[rid["keep"]]).start()
        for h in range(HT):
            for x_ in range(n_lx):
                dst = pl.ds(n_lx * toff[h] + x_ * tsz[h], tsz[h])
                src = span((ly * n_lx + x_) * D + toff[h], tsz[h], UNIT)
                pltpu.make_async_copy(tt.at[src, :], own_t.at[ly, dst, :], rs.at[rid["keep"]]).start()

    def teacher_kept():
        both = txt_s.at[pl.ds(0, D * (n_ly + n_lx) // n_loop), :]
        pltpu.make_async_copy(both, both, rs.at[rid["keep"]]).wait()

    teacher_keep()
    own_text(0)
    own_image(0)
    pl.semaphore_wait(barrier, n_peer)

    def teacher_exchange():
        for h in range(HI):
            for y_ in range(n_ly):
                dst = pl.ds(n_ly * ioff[h] + y_ * isz[h], isz[h])
                for e in range(1, n_lx):
                    x_ = (lx + e) % n_lx
                    src = span((y_ * n_lx + x_) * D + ioff[h], isz[h], UNIT)
                    send(ti.at[src, :], raw_i.at[kl, ly, lx, dst, :], "t_img", rid["t_img"], dev(lx_=x_))
        for h in range(HT):
            for x_ in range(n_lx):
                dst = pl.ds(n_lx * toff[h] + x_ * tsz[h], tsz[h])
                for e in range(1, n_ly):
                    y_ = (ly + e) % n_ly
                    src = span((y_ * n_lx + x_) * D + toff[h], tsz[h], UNIT)
                    send(tt.at[src, :], own_t.at[ly, dst, :], "t_txt", rid["t_txt"], dev(ly_=y_))

    moved_i = raw_i.at[0, 0, pl.ds(0, n_lx - 1)]
    moved_t = own_t.at[pl.ds(0, n_ly - 1)]

    def image_z(a, h):
        ref = image_ref(a, kl, ly, h)
        for d in range(1, n_kl):
            q = rid[("iz", a)] + d * HI + h
            send(ref, ref, ("img", a), q, dev(k_=kh * n_kl + (kl + d) % n_kl), isz[h])

    def image_y(a, h):
        ref = image_ref(a, kl, ly, h)
        for e in range(1, n_ly):
            send(ref, ref, ("img", a), rid[("iy", a)] + h, dev(ly_=(ly + e) % n_ly), isz[h])

    def image_relay(a, h):
        for d in range(1, n_kl):
            ref = image_ref(a, (kl + n_kl - d) % n_kl, ly, h)
            got(ref, rid[("iz", a)] + d * HI + h)
            for e in range(1, n_ly):
                send(ref, ref, ("img", a), rid[("iy", a)] + h, dev(ly_=(ly + e) % n_ly), isz[h])

    def image_finish(a, h):
        got_rows((n_ly - 1) * n_kl * isz[h], rid[("iy", a)] + h)
        if a == 0:
            return
        for p in range(n_kl):
            for y_ in range(n_ly):
                def load(o):
                    rng = pl.ds(n_ly * ioff[h] + y_ * isz[h] + o, UNIT)
                    xs = [raw_i[p, fy, fx, rng, :] for fy in range(n_ly) for fx in range(n_lx)]
                    return jnp.concatenate(xs, axis=1).astype(F32)
                unit(load, img_t, n_img * ioff[h] + islot(p, y_) * isz[h], isz[h])

    def text_first(a, h):
        src = own_ref(a, h)
        for g in range(n_kh):
            dest = g * n_kl + src_kl
            op = copy(src, text_ref(a, src_j, lx, h), sid[("first", a)],
                      rid[("tz", a)] + src_j * HT + h, dev(k_=dest))

            @pl.when(dest != k)
            def _():
                op.start()

            @pl.when(dest == k)
            def _():
                if a == 0:
                    txt_s[trng(h, tslot(src_j, lx, c)), :] = own_s[pl.ds(toff[h], tsz[h]), :]
                else:
                    rng = pl.ds(n_lx * toff[h], n_lx * tsz[h])
                    raw_t[src_j, lx, :, rng, :] = own_t[:, rng, :]

    def first_left(a):
        @pl.when(src_kl == kl)
        def _():
            left(txt_s.at[pl.ds(0, (n_kh - 1) * D), :], sid[("first", a)])

        @pl.when(src_kl != kl)
        def _():
            left(txt_s.at[pl.ds(0, n_kh * D), :], sid[("first", a)])

    def core_send(a, ref, h):
        send(ref, ref, ("txt", a), rid[("tc", a)] + h, dev(c_=1 - c), tsz[h])

    def text_relay(a, h):
        for j in range(n_kh):
            ref = text_ref(a, j, lx, h)

            @pl.when(kl * n_kh + j != k)
            def _():
                got(ref, rid[("tz", a)] + j * HT + h)

            for e in range(1, n_lx):
                send(ref, ref, ("txt", a), rid[("tx", a)] + e * HT + h, dev(lx_=(lx + e) % n_lx), tsz[h])
            if a == 0:
                core_send(a, ref, h)

    def text_cross(a, h):
        for e in range(1, n_lx):
            got_rows(n_kh * tsz[h], rid[("tx", a)] + e * HT + h)
            for j in range(n_kh):
                if a == 0:
                    core_send(a, text_ref(a, j, (lx + n_lx - e) % n_lx, h), h)
        if a == 0:
            return
        for j in range(n_kh):
            for x_ in range(n_lx):
                def load(o):
                    rng = pl.ds(n_lx * toff[h] + x_ * tsz[h] + o, UNIT)
                    xs = [raw_t[j, fx, fy, rng, :] for fy in range(n_ly) for fx in range(n_lx)]
                    return jnp.concatenate(xs, axis=1).astype(F32)
                unit(load, txt_t, n_txt * toff[h] + tslot(j, x_, c) * tsz[h], tsz[h])
                core_send(a, txt_t.at[trng(h, tslot(j, x_, c)), :], h)

    def text_finish(a, h):
        got_rows(n_lx * n_kh * tsz[h], rid[("tc", a)] + h)

    def tile_of(n, most):
        return max(t for t in range(UNIT, min(n, most) + 1, UNIT) if n % t == 0)

    def logits(txt, img, scale, out, row0, n):
        tile = tile_of(n, TILE)
        m = jnp.full((8, rows), -jnp.inf, F32)
        for o in range(row0, row0 + n, tile):
            v = scale * lax.dot_general(
                txt[pl.ds(o, tile), :], img[...], (((1,), (1,)), ((), ())),
                preferred_element_type=F32,
            )
            out[pl.ds(o, tile), :] = v
            m = jnp.maximum(m, jnp.max(v.reshape(tile // 8, 8, rows), axis=0))
        return jnp.max(m, axis=0, keepdims=True)

    def zipped(image_step, text_step):
        for h in range(max(HI, HT)):
            if h < HT:
                text_step(h)
            if h < HI:
                image_step(h)

    teacher_exchange()

    def student_text(h):
        if h:
            own_text(h)
        text_first(0, h)

    def student_image(h):
        if h:
            own_image(h)
        image_z(0, h)
        image_y(0, h)
    zipped(student_image, student_text)
    text_relay(0, 0)
    image_relay(0, 0)
    teacher_kept()
    got(moved_i, rid["t_img"])
    got(moved_t, rid["t_txt"])
    ahead = min(3, HT)
    for h in range(ahead):
        text_first(1, h)
    for h in range(max(HI, HT - ahead)):
        if h < HI:
            image_z(1, h)
        if ahead + h < HT:
            text_first(1, ahead + h)
    relay_s = [functools.partial(text_relay, 0, h) for h in range(1, HT)]
    relay_t = [functools.partial(text_relay, 1, h) for h in range(HT)]
    image_s = [functools.partial(image_relay, 0, h) for h in range(1, HI)]
    image_t = [functools.partial(image_relay, 1, h) for h in range(HI)]
    cross_s = [functools.partial(text_cross, 0, h) for h in range(HT)]
    cross_t = [functools.partial(text_cross, 1, h) for h in range(HT)]
    finish_t = [functools.partial(image_finish, 1, h) for h in range(HI)]

    def step(*queues):
        for queue in queues:
            if queue:
                queue.pop(0)()

    step(relay_s)
    while relay_s:
        step(image_s, relay_s, cross_s)
    while image_s:
        step(image_s)
    for h in range(HI):
        image_y(1, h)
    while len(cross_s) > 2:
        step(cross_s)
    step(relay_t)
    step(cross_s, cross_s)
    step(relay_t)
    while cross_s:
        step(cross_s)
    for h in range(HI):
        image_finish(0, h)
    for h in range(HT):
        text_finish(0, h)
    step(image_t)
    step(relay_t)
    smax = logits(txt_s, img_s, sscale, slog, 0, cols)
    step(cross_t)
    step(relay_t)
    step(image_t)
    step(cross_t)
    while len(image_t) > 0:
        step(image_t)
    while relay_t:
        step(relay_t)
    while len(cross_t) > 2:
        step(cross_t)
    step(finish_t)
    step(cross_t)
    while finish_t:
        step(finish_t)
    def exps(row0, n, top_t):
        def fold(v):
            return jnp.sum(v.reshape(STEP // 8, 8, rows), axis=0)

        def body(i, carry):
            a, b, x = carry
            o = pl.multiple_of(row0 + i * STEP, STEP)
            s = slog[pl.ds(o, STEP), :]
            t = tlog[pl.ds(o, STEP), :]
            es = jnp.exp(s - smax)
            et = jnp.exp(t - top_t)
            slog[pl.ds(o, STEP), :] = es
            tlog[pl.ds(o, STEP), :] = et
            return (a + fold(es), b + fold(et), x + fold(et * (t - s)))
        zero = jnp.zeros((8, rows), F32)
        return lax.fori_loop(0, n // STEP, body, (zero, zero, zero))

    row0 = [n_txt * o for o in toff]
    height = [n_txt * n for n in tsz]
    tops = []
    sums = []

    def teacher(h0, h1):
        for h in range(h0, h1):
            text_finish(1, h)
        n = sum(height[h0:h1])
        top = logits(txt_t, img_t, tscale, tlog, row0[h0], n)
        if h0 == 0:
            while cross_t:
                step(cross_t)
        tops.append(top)
        tops_at.extend([top] * (h1 - h0))
        sums.append([jnp.sum(v, axis=0, keepdims=True) for v in exps(row0[h0], n, top)])

    tops_at = []
    cuts = sorted({0, max(HT - 2, 0), HT - 1, HT})
    for h0, h1 in zip(cuts, cuts[1:]):
        teacher(h0, h1)

    tmax = functools.reduce(jnp.maximum, tops)
    shift = [jnp.exp(m - tmax) for m in tops]
    asum = sum(v[0] for v in sums)
    bsum = sum(v[1] * e for v, e in zip(sums, shift))
    xsum = sum(v[2] * e for v, e in zip(sums, shift))
    pack = [smax, tmax, asum, bsum, xsum]
    stat[islot(kl, ly)] = jnp.concatenate(pack + [jnp.zeros((3, rows), F32)], axis=0)
    for d in range(n_kl):
        for e in range(n_ly):
            if d or e:
                send(stat.at[islot(kl, ly)], stat.at[islot(kl, ly)], "stat", rid["stat"],
                     dev(k_=kh * n_kl + (kl + d) % n_kl, ly_=(ly + e) % n_ly))
    for a in range(2):
        first_left(a)
        left_rows(("img", a), ("txt", a))
    got(stat.at[pl.ds(0, n_img - 1)], rid["stat"])

    all_stat = [stat[s] for s in range(n_img)]
    gs = functools.reduce(jnp.maximum, [v[0:1] for v in all_stat])
    gt = functools.reduce(jnp.maximum, [v[1:2] for v in all_stat])
    es = [jnp.exp(v[0:1] - gs) for v in all_stat]
    et = [jnp.exp(v[1:2] - gt) for v in all_stat]
    ssum = sum(v[2:3] * e for v, e in zip(all_stat, es))
    tsum = sum(v[3:4] * e for v, e in zip(all_stat, et))
    cross = sum(v[4:5] * e for v, e in zip(all_stat, et))
    diverge = cross / tsum - (gt + jnp.log(tsum)) + (gs + jnp.log(ssum))
    mine = tslot(kh, lx, c)
    part[mine] = jnp.broadcast_to(jnp.sum(diverge, axis=1, keepdims=True), (8, 128))
    for peer in loss_peers:
        send(part.at[mine], part.at[mine], "loss", rid["loss"], loss_peer(*peer))

    s_mul = sscale * jnp.exp(smax - gs) / ssum
    t_scale = sscale / tsum

    t_mul = [t_scale * jnp.exp(m - gt) for m in tops_at]

    dtxt = txt_t

    def grad_of(rng, h):
        v = (slog[rng, :] * s_mul - tlog[rng, :] * t_mul[h]).astype(BF16)
        grad[rng, :] = v
        return v

    def text_piece(j, lx_, c_, fresh=False):
        slot = tslot(j, lx_, c_)
        if fresh:
            g = [grad_of(trng(h, slot), h) for h in range(HT)]
        else:
            g = [grad[trng(h, slot), :] for h in range(HT)]
        v = jnp.dot(jnp.concatenate(g, axis=0), img_s[...], preferred_element_type=F32)
        dtxt[at(slot), :] = v.astype(BF16)

    order = [(n_kh - 1 - kh + i) % n_kh for i in range(n_kh)]

    def to_core(e, i, fresh=False):
        x_ = (lx + e) % n_lx
        j = order[i]
        text_piece(j, x_, 1 - c, fresh)
        for h in range(HB):
            send(dtxt.at[brng(tslot(j, x_, 1 - c), h), :], r1.at[x_ * n_kh + j, part_of[h], :], "dc",
                 rid["dc"] + (e * n_kh + i) * HB + h, dev(c_=1 - c), bsz[h])

    def from_core(e, i, h):
        s = ((lx + e) % n_lx) * n_kh + order[i]
        got(r1.at[s, part_of[h], :], rid["dc"] + (e * n_kh + i) * HB + h)
        return r1[s, part_of[h], :].astype(F32)

    def to_x(e, i):
        x_ = (lx + e) % n_lx
        j = order[i]
        for h in range(HB):
            rng = brng(tslot(j, x_, c), h)
            dtxt[rng, :] = (dtxt[rng, :].astype(F32) + from_core(e, i, h)).astype(BF16)
            q = rid["dx"] + (e * n_kh + i) * HB + h
            send(dtxt.at[rng, :], r2.at[(e - 1) * n_kh + j, part_of[h], :], "dx", q, dev(lx_=x_), bsz[h])

    dimg = img_t
    full = [h for h in range(HI) if (n_kl * isz[h]) % 128 == 0]
    rest = [h for h in range(HI) if h not in full]

    def image_piece(y_, with_rest):
        windows = [span(n_img * ioff[h] + y_ * n_kl * isz[h], n_kl * isz[h], 128) for h in full]
        if with_rest:
            windows += [pl.ds(n_img * ioff[h], n_img * isz[h]) for h in rest]
        tile = tile_of(cols, DOT)
        wide = code if tile == cols else code // 2
        for n0 in range(0, code, wide):
            out = pl.ds(n0, wide)
            v = 0.0
            for o in range(0, cols, tile):
                g = jnp.concatenate([grad[pl.ds(o, tile), w] for w in windows], axis=1)
                v = v + lax.dot_general(
                    g, txt_s[pl.ds(o, tile), out], (((0,), (0,)), ((), ())), preferred_element_type=F32,
                )
            v = v.astype(BF16)
            slots = [(islot(p, y_), h) for h in full for p in range(n_kl)]
            if with_rest:
                slots += [(s, h) for h in rest for s in range(n_img)]
            o = 0
            for s, h in slots:
                dimg[span(s * D + ioff[h], isz[h], UNIT), out] = v[o:o + isz[h]]
                o += isz[h]

    def to_y(e):
        y_ = (ly + e) % n_ly
        image_piece(y_, e == 1)
        for d in [*range(1, n_kl), 0]:
            for h in range(HB):
                q = rid["gy"] + d * HB + h
                send(dimg.at[brng(islot((kl + d) % n_kl, y_), h), :], ry.at[(e - 1) * n_kl + d, part_of[h], :],
                     "gy", q, dev(ly_=y_), bsz[h])

    x1 = (lx + 1) % n_lx
    to_core(1, 0, True)
    text_piece(order[0], x1, c, True)
    for h in range(HT):
        def to_grad(i, _):
            grad_of(span(row0[h] + i * STEP, STEP, STEP), h)
            return 0
        lax.fori_loop(0, height[h] // STEP, to_grad, 0, unroll=2)
    to_x(1, 0)
    to_core(0, 0)
    text_piece(order[0], lx, c)
    for e in range(1, n_ly):
        to_y(e)

    def owner_copy(i, h):
        j = order[i]
        dest = kl * n_kh + j
        op = copy(dtxt.at[brng(tslot(j, lx, c), h), :], r3.at[kh, part_of[h], :], sid["dz"], rid["dz"], dev(k_=dest))
        return dest, op

    def text_sum(i, h):
        j = order[i]
        rng = brng(tslot(j, lx, c), h)
        v = dtxt[rng, :].astype(F32) + from_core(0, i, h)
        for e in range(1, n_lx):
            got(r2.at[(e - 1) * n_kh + j, part_of[h], :], rid["dx"] + (e * n_kh + i) * HB + h)
            v = v + r2[(e - 1) * n_kh + j, part_of[h], :].astype(F32)
        dtxt[rng, :] = v.astype(BF16)
        dest, op = owner_copy(i, h)

        @pl.when(dest != k)
        def _():
            op.start()

        @pl.when(dest == k)
        def _():
            r3[kh, part_of[h], :] = dtxt[rng, :]

    def got_y(d, h):
        got_rows((n_ly - 1) * bsz[h], rid["gy"] + d * HB + h)

    def image_sum(d, h):
        got_y(d, h)
        rng = brng(islot((kl + d) % n_kl, ly), h)
        v = dimg[rng, :].astype(F32)
        for e in range(1, n_ly):
            v = v + ry[(e - 1) * n_kl + d, part_of[h], :].astype(F32)
        dimg[rng, :] = v.astype(BF16)
        send(dimg.at[rng, :], rz.at[d - 1, part_of[h], :], "gz", rid["gz"], dev(k_=kh * n_kl + (kl + d) % n_kl), bsz[h])

    text_sum(0, 0)
    for e in range(1, n_lx):
        for i in range(1 if e == 1 else 0, n_kh):
            to_core(e, i)
            text_piece(order[i], (lx + e) % n_lx, c)
            if e > 1 or i > 1:
                to_x(e, i)
    image_piece(ly, n_ly == 1)
    if n_kh > 1:
        to_x(1, 1)
    texts = [(i, h) for i in range(n_kh) for h in range(HB)][1:]
    images = [(d, h) for d in range(1, n_kl) for h in range(HB)]
    while texts or images:
        if texts:
            i, h = texts.pop(0)
            if h == HB - 1 and i + 1 < n_kh:
                to_core(0, i + 1)
                text_piece(order[i + 1], lx, c)
            text_sum(i, h)
        if images:
            image_sum(*images.pop(0))
    got(part.at[pl.ds(0, len(loss_peers))], rid["loss"])
    loss_out[...] = sum(part[i] for i in range(n_txt)) / float(D * n_row * n_loop)

    def finish(terms, src, inv_ref, out):
        for o in range(0, D, UNIT):
            rng = pl.ds(o, UNIT)
            g = terms(o)
            x = src[rng, :].astype(F32)
            inv = inv_ref[rng, 0:1]
            along = jnp.sum(g * x, axis=1, keepdims=True) * inv * inv
            out[rng, :] = ((g - x * along) * inv).astype(BF16)

    for h in range(HB):
        got_y(0, h)
    got_rows((n_kl - 1) * D, rid["gz"])

    def image_terms(o):
        v = dimg[span(islot(kl, ly) * D + o, UNIT, UNIT), :].astype(F32)
        for e in range(1, n_ly):
            v = v + ry[(e - 1) * n_kl, pl.ds(o, UNIT), :].astype(F32)
        for d in range(1, n_kl):
            v = v + rz[d - 1, pl.ds(o, UNIT), :].astype(F32)
        return v
    finish(image_terms, si, inv_i, gi_out)

    def on_owner(wait):
        @pl.when(src_kl == kl)
        def _():
            wait(n_kh - 1)

        @pl.when(src_kl != kl)
        def _():
            wait(n_kh)
    on_owner(lambda n: got(txt_s.at[pl.ds(0, n * D), :], rid["dz"]))
    finish(lambda o: sum(r3[g, pl.ds(o, UNIT), :].astype(F32) for g in range(n_kh)), st, inv_t, gt_out)

    left(moved_i, sid["t_img"])
    left(moved_t, sid["t_txt"])
    left(stat.at[pl.ds(0, n_img - 1)], sid["stat"])
    left_rows("dc", "dx", "gy", "gz")
    left(part.at[pl.ds(0, len(loss_peers))], sid["loss"])

    on_owner(lambda n: left(txt_s.at[pl.ds(0, n * D), :], sid["dz"]))


def emit(total, gi, gt, loss_out, gi_out, gt_out):
    loss_out[0] = total[0, 0]
    gi_out[...] = gi[...]
    gt_out[...] = gt[...]


def on_device(n_row, n_loop, si, st, ti, tt, ssc, tsc):
    D, code = si.shape
    n_kl, n_lx = 2, 2
    n_kh, n_ly = n_row // (2 * n_kl), n_loop // n_lx
    n_img, n_txt = n_kl * n_ly, n_kh * n_lx * 2
    rows, cols = n_img * D, n_txt * D
    feat = code // n_loop
    rid, sid = make_ids(D, n_kh, n_kl, n_lx, n_ly)
    dims = (n_row, n_loop, n_kh, n_kl, n_lx, n_ly, D, code)
    vm = pl.BlockSpec(memory_space=pltpu.VMEM)
    sm = pl.BlockSpec(memory_space=pltpu.SMEM)
    anywhere = pl.BlockSpec(memory_space=pl.ANY)
    V = pltpu.VMEM
    loss, gi, gt = pl.pallas_call(
        functools.partial(kernel, dims, rid, sid),
        out_shape=(
            jax.ShapeDtypeStruct((8, 128), F32),
            jax.ShapeDtypeStruct((D, code), BF16),
            jax.ShapeDtypeStruct((D, code), BF16),
        ),
        in_specs=[vm, vm, anywhere, anywhere, sm, sm],
        out_specs=(vm, vm, vm),
        scratch_shapes=[
            V((rows, code), BF16), V((rows, code), BF16),
            V((D, code), BF16), V((n_ly, n_lx * D, feat), BF16),
            V((cols, code), BF16), V((cols, code), BF16),
            V((n_kl, n_ly, n_lx, n_ly * D, feat), BF16),
            V((n_kh, n_lx, n_ly, n_lx * D, feat), BF16),
            V((cols, rows), F32), V((cols, rows), F32), V((cols, rows), BF16),
            V((n_img, 8, rows), F32),
            V((n_lx * n_kh, D, code), BF16),
            V(((n_lx - 1) * n_kh, D, code), BF16),
            V((n_kh, D, code), BF16),
            V(((n_ly - 1) * n_kl, D, code), BF16),
            V((n_kl - 1, D, code), BF16),
            V((n_txt, 8, 128), F32),
            V((D, 128), F32), V((D, 128), F32),
            pltpu.SemaphoreType.DMA((sid.count,)),
            pltpu.SemaphoreType.DMA((rid.count,)),
        ],
        compiler_params=pltpu.CompilerParams(
            collective_id=0, has_side_effects=True, vmem_limit_bytes=67043328,
        ),
    )(si, st, ti, tt, ssc, tsc)
    return pl.pallas_call(
        emit,
        out_shape=(
            jax.ShapeDtypeStruct((1,), F32),
            jax.ShapeDtypeStruct((D, code), BF16),
            jax.ShapeDtypeStruct((D, code), BF16),
        ),
        in_specs=[vm] * 3,
        out_specs=(sm, vm, vm),
    )(loss, gi, gt)


def solution(mesh):
    return jax.shard_map(
        functools.partial(on_device, mesh.shape["row"], mesh.shape["loop"]),
        mesh=mesh,
        in_specs=(
            P(("row", "loop"), None),
            P(("row", "loop"), None),
            P("row", "loop"),
            P("row", "loop"),
            P(),
            P(),
        ),
        out_specs=(P(), P(("row", "loop"), None), P(("row", "loop"), None)),
        check_vma=False,
    )
```

time: 82.1 us -> 79.2 us (0.965)
  Pallas kernels: 79.9 us -> 77.1 us
    pallas_call x1, Pallas kernels: 78 us -> 75.1 us  [on_device(): pl.pallas_call(functools.partial(kernel, dims, rid, sid), out_shape=(jax....]
where the time goes in v4:
time: 79.2 us; the launch traced here: 79 us
  Pallas kernels  77.1 us (97%)
  between operations  1.93 us (2%)
    pallas_call x1, Pallas kernels, on_device(): pl.pallas_call(functools.partial(kernel, dims, rid, sid), out_shape=(jax....  75.1 us
    pallas_call x1, Pallas kernels, on_device(): pl.pallas_call(emit, out_shape=(jax.ShapeDtypeStruct((1,), F32), jax.Shap...  1.94 us

profile of v4, /device:TPU:0, one launch (start us, length us, event | category | flops | bytes accessed | tf_op | source)
XLA Modules:
  0.0 79.0 jit_solution(2418051309006419644)
XLA Ops:
  1.9 75.1 %shard_map.85 = (f32[8,128]{1,0:T(8,128)}, bf16[160,1024]{1,0:T(8,128)(2,1)}, bf16[160,1024]{1,0:T(8,128)(2,1)}) custom-call(bf16[160,1024]{1,0:T(8,128)(2,1)} %si.1, bf16[160,1024]{1,0:T(8,128)(2,1)} %st.1, bf16[640,256]{1,0:T(8,128)(2,1)} %ti.1, bf16[640,256]{1,0:T(8,128)(2,1)} %tt.1, f32[1]{0:T(128)S(6)} %copy.9.ssc, f32[1]{0:T(128)S(6)} %copy.10.tsc), custom_call_target="tpu_custom_call" | custom-call | tf_op jit(solution)/shard_map/pallas_call | solution.py:739
  77.1 1.9 %shard_map.86 = (f32[1]{0:T(128)}, bf16[160,1024]{1,0:T(8,128)(2,1)}, bf16[160,1024]{1,0:T(8,128)(2,1)}) custom-call(f32[8,128]{1,0:T(8,128)} %get-tuple-element.6.total, bf16[160,1024]{1,0:T(8,128)(2,1)} %get-tuple-element.7.gi, bf16[160,1024]{1,0:T(8,128)(2,1)} %get-tuple-element.8.gt), custom_call_target="tpu_custom_call" | custom-call | tf_op jit(solution)/shard_map/pallas_call | solution.py:770

commit v5 on v4

--- a/solution.py
+++ b/solution.py
@@ -51,19 +51,20 @@
     recv.take("t_img")
     recv.take("t_txt")
     for a in range(2):
-        recv.take(("iz", a), n_kl * HI)
+        recv.take(("iz", a), (n_kl - 1) * HI)
         recv.take(("iy", a), HI)
         recv.take(("tz", a), n_kh * HT)
-        recv.take(("tx", a), n_lx * HT)
+        recv.take(("tx", a), (n_lx - 1) * HT)
         recv.take(("tc", a), HT)
     recv.take("stat")
-    recv.take("dc", n_lx * n_kh * HB)
-    recv.take("dx", n_lx * n_kh * HB)
+    recv.take("dc", n_lx * n_kh - 1 + HB)
+    recv.take("dx", (n_lx - 1) * n_kh * HB)
     recv.take("dz")
     recv.take("gy", n_kl * HB)
     recv.take("gz")
     recv.take("loss")
     recv.take("keep")
+    recv.take("load", 2)
     for name in ("t_img", "t_txt", "stat", "dc", "dx", "dz", "gy", "gz", "loss"):
         sent.take(name)
     for a in range(2):
@@ -74,10 +75,10 @@
 
 def kernel(
     dims, rid, sid,
-    si, st, ti, tt, ssc, tsc,
+    si_in, st_in, ti, tt, ssc, tsc,
     loss_out, gi_out, gt_out,
     img_s, img_t, own_s, own_t, txt_s, txt_t, raw_i, raw_t,
-    slog, tlog, grad, stat, r1, r2, r3, ry, rz, part, inv_i, inv_t,
+    slog, tlog, grad, stat, r1, r2, r3, ry, rz, part, inv_i, inv_t, si, st,
     ss, rs,
 ):
     n_row, n_loop, n_kh, n_kl, n_lx, n_ly, D, code = dims
@@ -236,8 +237,14 @@
         both = txt_s.at[pl.ds(0, D * (n_ly + n_lx) // n_loop), :]
         pltpu.make_async_copy(both, both, rs.at[rid["keep"]]).wait()
 
+    load_t = pltpu.make_async_copy(st_in, st, rs.at[rid["load"]])
+    load_i = pltpu.make_async_copy(si_in, si, rs.at[rid["load"] + 1])
+    load_t.start()
+    load_i.start()
     teacher_keep()
+    load_t.wait()
     own_text(0)
+    load_i.wait()
     own_image(0)
     pl.semaphore_wait(barrier, n_peer)
 
@@ -263,7 +270,7 @@
     def image_z(a, h):
         ref = image_ref(a, kl, ly, h)
         for d in range(1, n_kl):
-            q = rid[("iz", a)] + d * HI + h
+            q = rid[("iz", a)] + (d - 1) * HI + h
             send(ref, ref, ("img", a), q, dev(k_=kh * n_kl + (kl + d) % n_kl), isz[h])
 
     def image_y(a, h):
@@ -274,7 +281,7 @@
     def image_relay(a, h):
         for d in range(1, n_kl):
             ref = image_ref(a, (kl + n_kl - d) % n_kl, ly, h)
-            got(ref, rid[("iz", a)] + d * HI + h)
+            got(ref, rid[("iz", a)] + (d - 1) * HI + h)
             for e in range(1, n_ly):
                 send(ref, ref, ("img", a), rid[("iy", a)] + h, dev(ly_=(ly + e) % n_ly), isz[h])
 
@@ -330,13 +337,13 @@
                 got(ref, rid[("tz", a)] + j * HT + h)
 
             for e in range(1, n_lx):
-                send(ref, ref, ("txt", a), rid[("tx", a)] + e * HT + h, dev(lx_=(lx + e) % n_lx), tsz[h])
+                send(ref, ref, ("txt", a), rid[("tx", a)] + (e - 1) * HT + h, dev(lx_=(lx + e) % n_lx), tsz[h])
             if a == 0:
                 core_send(a, ref, h)
 
     def text_cross(a, h):
         for e in range(1, n_lx):
-            got_rows(n_kh * tsz[h], rid[("tx", a)] + e * HT + h)
+            got_rows(n_kh * tsz[h], rid[("tx", a)] + (e - 1) * HT + h)
             for j in range(n_kh):
                 if a == 0:
                     core_send(a, text_ref(a, j, (lx + n_lx - e) % n_lx, h), h)
@@ -543,17 +550,33 @@
 
     order = [(n_kh - 1 - kh + i) % n_kh for i in range(n_kh)]
 
+    def core_id(e, i):
+        first = n_kh if n_lx > 1 else 0
+        n = e * n_kh + i
+        if n == first:
+            return rid["dc"] + n_lx * n_kh - 1
+        return rid["dc"] + (n if n < first else n - 1)
+
+    def chunked(e, i):
+        return e == (1 if n_lx > 1 else 0) and i == 0
+
     def to_core(e, i, fresh=False):
         x_ = (lx + e) % n_lx
         j = order[i]
         text_piece(j, x_, 1 - c, fresh)
-        for h in range(HB):
-            send(dtxt.at[brng(tslot(j, x_, 1 - c), h), :], r1.at[x_ * n_kh + j, part_of[h], :], "dc",
-                 rid["dc"] + (e * n_kh + i) * HB + h, dev(c_=1 - c), bsz[h])
+        if chunked(e, i):
+            for h in range(HB):
+                send(dtxt.at[brng(tslot(j, x_, 1 - c), h), :], r1.at[x_ * n_kh + j, part_of[h], :], "dc",
+                     core_id(e, i) + h, dev(c_=1 - c), bsz[h])
+        else:
+            send(dtxt.at[at(tslot(j, x_, 1 - c)), :], r1.at[x_ * n_kh + j], "dc", core_id(e, i), dev(c_=1 - c), D)
 
     def from_core(e, i, h):
         s = ((lx + e) % n_lx) * n_kh + order[i]
-        got(r1.at[s, part_of[h], :], rid["dc"] + (e * n_kh + i) * HB + h)
+        if chunked(e, i):
+            got(r1.at[s, part_of[h], :], core_id(e, i) + h)
+        elif h == 0:
+            got(r1.at[s], core_id(e, i))
         return r1[s, part_of[h], :].astype(F32)
 
     def to_x(e, i):
@@ -562,7 +585,7 @@
         for h in range(HB):
             rng = brng(tslot(j, x_, c), h)
             dtxt[rng, :] = (dtxt[rng, :].astype(F32) + from_core(e, i, h)).astype(BF16)
-            q = rid["dx"] + (e * n_kh + i) * HB + h
+            q = rid["dx"] + ((e - 1) * n_kh + i) * HB + h
             send(dtxt.at[rng, :], r2.at[(e - 1) * n_kh + j, part_of[h], :], "dx", q, dev(lx_=x_), bsz[h])
 
     dimg = img_t
@@ -626,7 +649,7 @@
         rng = brng(tslot(j, lx, c), h)
         v = dtxt[rng, :].astype(F32) + from_core(0, i, h)
         for e in range(1, n_lx):
-            got(r2.at[(e - 1) * n_kh + j, part_of[h], :], rid["dx"] + (e * n_kh + i) * HB + h)
+            got(r2.at[(e - 1) * n_kh + j, part_of[h], :], rid["dx"] + ((e - 1) * n_kh + i) * HB + h)
             v = v + r2[(e - 1) * n_kh + j, part_of[h], :].astype(F32)
         dtxt[rng, :] = v.astype(BF16)
         dest, op = owner_copy(i, h)
@@ -743,7 +766,7 @@
             jax.ShapeDtypeStruct((D, code), BF16),
             jax.ShapeDtypeStruct((D, code), BF16),
         ),
-        in_specs=[vm, vm, anywhere, anywhere, sm, sm],
+        in_specs=[anywhere] * 4 + [sm] * 2,
         out_specs=(vm, vm, vm),
         scratch_shapes=[
             V((rows, code), BF16), V((rows, code), BF16),
@@ -760,6 +783,7 @@
             V((n_kl - 1, D, code), BF16),
             V((n_txt, 8, 128), F32),
             V((D, 128), F32), V((D, 128), F32),
+            V((D, code), BF16), V((D, code), BF16),
             pltpu.SemaphoreType.DMA((sid.count,)),
             pltpu.SemaphoreType.DMA((rid.count,)),
         ],

time: 79.2 us -> 78 us (0.985)
  Pallas kernels: 77.1 us -> 75.9 us
    pallas_call x1, Pallas kernels: 75.1 us -> 73.9 us  [on_device(): pl.pallas_call(functools.partial(kernel, dims, rid, sid), out_shape=(jax....]
where the time goes in v5:
time: 78 us; the launch traced here: 77.8 us
  Pallas kernels  75.9 us (97%)
  between operations  1.93 us (2%)
    pallas_call x1, Pallas kernels, on_device(): pl.pallas_call(functools.partial(kernel, dims, rid, sid), out_shape=(jax....  73.9 us
    pallas_call x1, Pallas kernels, on_device(): pl.pallas_call(emit, out_shape=(jax.ShapeDtypeStruct((1,), F32), jax.Shap...  1.94 us

profile of v5, /device:TPU:0, one launch (start us, length us, event | category | flops | bytes accessed | tf_op | source)
XLA Modules:
  0.0 77.8 jit_solution(610681819362613059)
XLA Ops:
  1.9 73.9 %shard_map.85 = (f32[8,128]{1,0:T(8,128)}, bf16[160,1024]{1,0:T(8,128)(2,1)}, bf16[160,1024]{1,0:T(8,128)(2,1)}) custom-call(bf16[160,1024]{1,0:T(8,128)(2,1)} %si_in.1, bf16[160,1024]{1,0:T(8,128)(2,1)} %st_in.1, bf16[640,256]{1,0:T(8,128)(2,1)} %ti.1, bf16[640,256]{1,0:T(8,128)(2,1)} %tt.1, f32[1]{0:T(128)S(6)} %copy.9.ssc, f32[1]{0:T(128)S(6)} %copy.10.tsc), custom_call_target="tpu_custom_call" | custom-call | tf_op jit(solution)/shard_map/pallas_call | solution.py:762
  75.9 1.9 %shard_map.86 = (f32[1]{0:T(128)}, bf16[160,1024]{1,0:T(8,128)(2,1)}, bf16[160,1024]{1,0:T(8,128)(2,1)}) custom-call(f32[8,128]{1,0:T(8,128)} %get-tuple-element.6.total, bf16[160,1024]{1,0:T(8,128)(2,1)} %get-tuple-element.7.gi, bf16[160,1024]{1,0:T(8,128)(2,1)} %get-tuple-element.8.gt), custom_call_target="tpu_custom_call" | custom-call | tf_op jit(solution)/shard_map/pallas_call | solution.py:794

commit v6 on v5

--- a/solution.py
+++ b/solution.py
@@ -364,16 +364,17 @@
     def tile_of(n, most):
         return max(t for t in range(UNIT, min(n, most) + 1, UNIT) if n % t == 0)
 
-    def logits(txt, img, scale, out, row0, n):
+    def logits(txt, img, scale, out, row0, n, lane0=0, width=rows):
         tile = tile_of(n, TILE)
-        m = jnp.full((8, rows), -jnp.inf, F32)
+        lanes = pl.ds(lane0, width)
+        m = jnp.full((8, width), -jnp.inf, F32)
         for o in range(row0, row0 + n, tile):
             v = scale * lax.dot_general(
-                txt[pl.ds(o, tile), :], img[...], (((1,), (1,)), ((), ())),
+                txt[pl.ds(o, tile), :], img[lanes, :], (((1,), (1,)), ((), ())),
                 preferred_element_type=F32,
             )
-            out[pl.ds(o, tile), :] = v
-            m = jnp.maximum(m, jnp.max(v.reshape(tile // 8, 8, rows), axis=0))
+            out[pl.ds(o, tile), lanes] = v
+            m = jnp.maximum(m, jnp.max(v.reshape(tile // 8, 8, width), axis=0))
         return jnp.max(m, axis=0, keepdims=True)
 
     def zipped(image_step, text_step):
@@ -401,7 +402,7 @@
     teacher_kept()
     got(moved_i, rid["t_img"])
     got(moved_t, rid["t_txt"])
-    ahead = min(3, HT)
+    ahead = min(2, HT)
     for h in range(ahead):
         text_first(1, h)
     for h in range(max(HI, HT - ahead)):
@@ -443,58 +444,74 @@
     step(image_t)
     step(relay_t)
     smax = logits(txt_s, img_s, sscale, slog, 0, cols)
+    step(image_t)
     step(cross_t)
     step(relay_t)
     step(image_t)
     step(cross_t)
-    while len(image_t) > 0:
+    while image_t:
         step(image_t)
     while relay_t:
         step(relay_t)
     while len(cross_t) > 2:
         step(cross_t)
-    step(finish_t)
-    step(cross_t)
-    while finish_t:
-        step(finish_t)
-    def exps(row0, n, top_t):
+
+    def exps(row0, n, top_t, lane0=0, width=rows):
+        lanes = pl.ds(lane0, width)
+        top_s = smax[:, lane0:lane0 + width]
+
         def fold(v):
-            return jnp.sum(v.reshape(STEP // 8, 8, rows), axis=0)
+            return jnp.sum(v.reshape(STEP // 8, 8, width), axis=0)
 
         def body(i, carry):
             a, b, x = carry
             o = pl.multiple_of(row0 + i * STEP, STEP)
-            s = slog[pl.ds(o, STEP), :]
-            t = tlog[pl.ds(o, STEP), :]
-            es = jnp.exp(s - smax)
+            s = slog[pl.ds(o, STEP), lanes]
+            t = tlog[pl.ds(o, STEP), lanes]
+            es = jnp.exp(s - top_s)
             et = jnp.exp(t - top_t)
-            slog[pl.ds(o, STEP), :] = es
-            tlog[pl.ds(o, STEP), :] = et
+            slog[pl.ds(o, STEP), lanes] = es
+            tlog[pl.ds(o, STEP), lanes] = et
             return (a + fold(es), b + fold(et), x + fold(et * (t - s)))
-        zero = jnp.zeros((8, rows), F32)
-        return lax.fori_loop(0, n // STEP, body, (zero, zero, zero))
+        zero = jnp.zeros((8, width), F32)
+        sums = lax.fori_loop(0, n // STEP, body, (zero, zero, zero))
+        return [jnp.sum(v, axis=0, keepdims=True) for v in sums]
 
     row0 = [n_txt * o for o in toff]
     height = [n_txt * n for n in tsz]
     tops = []
     sums = []
 
-    def teacher(h0, h1):
-        for h in range(h0, h1):
-            text_finish(1, h)
-        n = sum(height[h0:h1])
-        top = logits(txt_t, img_t, tscale, tlog, row0[h0], n)
-        if h0 == 0:
-            while cross_t:
-                step(cross_t)
+    tops_at = []
+
+    def keep_stats(top, sums_, n):
         tops.append(top)
-        tops_at.extend([top] * (h1 - h0))
-        sums.append([jnp.sum(v, axis=0, keepdims=True) for v in exps(row0[h0], n, top)])
-
-    tops_at = []
-    cuts = sorted({0, max(HT - 2, 0), HT - 1, HT})
-    for h0, h1 in zip(cuts, cuts[1:]):
-        teacher(h0, h1)
+        tops_at.extend([top] * n)
+        sums.append(sums_)
+
+    def teacher(h):
+        text_finish(1, h)
+        top = logits(txt_t, img_t, tscale, tlog, row0[h], height[h])
+        keep_stats(top, exps(row0[h], height[h], top), 1)
+
+    first = max(HT - 3, 1)
+    n0 = sum(height[:first])
+    for h in range(first):
+        text_finish(1, h)
+    parts = []
+    for i in range(HI):
+        step(finish_t)
+        window = (n_img * ioff[i], n_img * isz[i])
+        top = logits(txt_t, img_t, tscale, tlog, 0, n0, *window)
+        parts.append([top] + exps(0, n0, top, *window))
+        if i + 2 == HI and len(cross_t) > 1:
+            step(cross_t)
+    parts = [jnp.concatenate(v, axis=1) for v in zip(*parts)]
+    keep_stats(parts[0], parts[1:], first)
+    for h in range(first, HT):
+        teacher(h)
+        while h == first and cross_t:
+            step(cross_t)
 
     tmax = functools.reduce(jnp.maximum, tops)
     shift = [jnp.exp(m - tmax) for m in tops]

time: 78 us -> 76.5 us (0.981)
  Pallas kernels: 75.9 us -> 74.4 us
    pallas_call x1, Pallas kernels: 73.9 us -> 72.5 us  [on_device(): pl.pallas_call(functools.partial(kernel, dims, rid, sid), out_shape=(jax....]
where the time goes in v6:
time: 76.5 us; the launch traced here: 76.4 us
  Pallas kernels  74.4 us (97%)
  between operations  1.93 us (3%)
    pallas_call x1, Pallas kernels, on_device(): pl.pallas_call(functools.partial(kernel, dims, rid, sid), out_shape=(jax....  72.5 us
    pallas_call x1, Pallas kernels, on_device(): pl.pallas_call(emit, out_shape=(jax.ShapeDtypeStruct((1,), F32), jax.Shap...  1.94 us

profile of v6, /device:TPU:0, one launch (start us, length us, event | category | flops | bytes accessed | tf_op | source)
XLA Modules:
  0.0 76.4 jit_solution(5457358163479417806)
XLA Ops:
  1.9 72.5 %shard_map.85 = (f32[8,128]{1,0:T(8,128)}, bf16[160,1024]{1,0:T(8,128)(2,1)}, bf16[160,1024]{1,0:T(8,128)(2,1)}) custom-call(bf16[160,1024]{1,0:T(8,128)(2,1)} %si_in.1, bf16[160,1024]{1,0:T(8,128)(2,1)} %st_in.1, bf16[640,256]{1,0:T(8,128)(2,1)} %ti.1, bf16[640,256]{1,0:T(8,128)(2,1)} %tt.1, f32[1]{0:T(128)S(6)} %copy.9.ssc, f32[1]{0:T(128)S(6)} %copy.10.tsc), custom_call_target="tpu_custom_call" | custom-call | tf_op jit(solution)/shard_map/pallas_call | solution.py:779
  74.4 1.9 %shard_map.86 = (f32[1]{0:T(128)}, bf16[160,1024]{1,0:T(8,128)(2,1)}, bf16[160,1024]{1,0:T(8,128)(2,1)}) custom-call(f32[8,128]{1,0:T(8,128)} %get-tuple-element.6.total, bf16[160,1024]{1,0:T(8,128)(2,1)} %get-tuple-element.7.gi, bf16[160,1024]{1,0:T(8,128)(2,1)} %get-tuple-element.8.gt), custom_call_target="tpu_custom_call" | custom-call | tf_op jit(solution)/shard_map/pallas_call | solution.py:811
